TPU v7x, 128 devices: a whole 4x4x4 slice. The times are simulated.
128 devices in a mesh: tm: 4 (over x), space: 32 (over z, y, core).
Axes of the slice: x: 4, y: 4, z: 4, core: 2. Of those that a mesh axis runs over, the one named last changes fastest.
Arguments:
- source: float32 [32, 2048, 1024], P('tm', 'space'), may hold values from -6 to 6
- guess: float32 [32, 2048, 1024], P('tm', 'space'), may hold values from -6 to 6
- start_state: float32 [2048, 1024], P('space'), may hold values from -6 to 6
- conduct: float32 [2048, 1024], P('space'), may hold values from 0.5 to 4
Outputs:
- solution_field: float32 [32, 2048, 1024], P('tm', 'space')
- residual: float32 [32, 2048, 1024], P('tm', 'space')
All inputs are finite; a program needn't handle non-finite values.
Results may differ from a plain program's by a relative error of at most 0.00002.
Values sent between devices are 32-bit elements; how exact they have to be, the bound alone decides.
A program may use at most 64 MiB of HBM per device.

v0:
```python
import jax
import jax.numpy as jnp
from jax import lax
from jax.sharding import PartitionSpec as P

damping = 0.8


def extended(cells, sides, width):
    for axis, dim in sides:
        count = lax.axis_size(axis)
        ends = count - 1
        head = lax.slice_in_dim(cells, 0, width, axis=dim)
        tail = lax.slice_in_dim(cells, cells.shape[dim] - width, cells.shape[dim], axis=dim)
        cells = jnp.concatenate(
            [
                lax.ppermute(tail, axis, [(i, (i + 1) % count) for i in range(ends)]),
                cells,
                lax.ppermute(head, axis, [((i + 1) % count, i) for i in range(ends)]),
            ],
            axis=dim,
        )
    return cells


def passed_along(block, axis, distance):
    devices = range(lax.axis_size(axis))
    route = [(i - distance, i) for i in devices if i - distance in devices]
    return lax.ppermute(block, axis, route)


def apply_operator(field, conduct):
    rimmed = extended(field, (("space", 1),), 1)
    padded = jnp.pad(rimmed, ((0, 0), (0, 0), (1, 1)))
    beside = padded[:, 2:, 1:-1] + padded[:, :-2, 1:-1] + padded[:, 1:-1, 2:] + padded[:, 1:-1, :-2]
    return field + conduct * (4.0 * field - beside)


def approx_inverse(resid, conduct):
    diagonal = 1.0 + 4.0 * conduct
    first_sweep = resid / diagonal
    return first_sweep + (resid - apply_operator(first_sweep, conduct)) / diagonal


def fine_residual(field, before, source, conduct):
    earlier = jnp.concatenate([before[None], field[:-1]], axis=0)
    return source + earlier - apply_operator(field, conduct)


def coarse_before(coarse):
    boundary = passed_along(coarse[-1], "tm", 1)
    return jnp.concatenate([boundary[None], coarse[:-1]], axis=0)


def apply_inner(widened, cond_wide):
    padded = jnp.pad(widened, ((0, 0), (0, 0), (1, 1)))
    centre = widened[:, 1:-1]
    beside = widened[:, 2:] + widened[:, :-2] + padded[:, 1:-1, 2:] + padded[:, 1:-1, :-2]
    return centre + cond_wide[1:-1] * (4.0 * centre - beside)


def widened_smooth(field, earlier, rhs, cond_wide, inside_mask):
    stacked = jnp.stack([field, earlier, rhs], axis=0)
    widened = extended(stacked, (("space", 2),), 2)
    resid_wide = widened[2][:, 1:-1] + widened[1][:, 1:-1] - apply_inner(widened[0], cond_wide)
    resid_wide = resid_wide * inside_mask
    cond_mid = cond_wide[1:-1]
    diagonal = 1.0 + 4.0 * cond_mid
    first_sweep = resid_wide / diagonal
    image = apply_inner(first_sweep, cond_mid)
    return first_sweep[:, 1:-1] + (resid_wide[:, 1:-1] - image) / diagonal[1:-1]


def shards(source, guess, start_state, conduct):
    is_first = lax.axis_index("tm") == 0

    def fine_before(field):
        boundary = passed_along(field[-1], "tm", 1)
        return jnp.where(is_first, start_state, boundary)

    half_steps = source.shape[0] // 2
    coarse_cond = 2.0 * conduct
    before0 = fine_before(guess)
    local_rows = conduct.shape[0]
    cond_wide = extended(conduct, (("space", 0),), 2)
    coarse_wide = 2.0 * cond_wide
    row_index = jnp.arange(local_rows + 2) + lax.axis_index("space") * local_rows - 1
    inside = (row_index >= 0) & (row_index < local_rows * lax.axis_size("space"))
    inside_mask = inside.astype(jnp.float32)[:, None]
    earlier0 = jnp.concatenate([before0[None], guess[:-1]], axis=0)
    smooth1 = guess + damping * widened_smooth(guess, earlier0, source, cond_wide, inside_mask)
    before1 = fine_before(smooth1)
    resid1 = fine_residual(smooth1, before1, source, conduct)
    pairs = resid1.reshape(half_steps, 2, source.shape[1], source.shape[2])
    restricted = pairs[:, 0] + pairs[:, 1]
    correction = damping * approx_inverse(restricted, coarse_cond)
    for sweep in range(2):
        earlier_coarse = coarse_before(correction)
        correction = correction + damping * widened_smooth(
            correction, earlier_coarse, restricted, coarse_wide, inside_mask
        )
    shifted_final = coarse_before(correction)
    even_steps = 0.5 * (shifted_final + correction)
    fine_corr = jnp.stack([even_steps, correction], axis=1).reshape(source.shape)
    smooth2 = smooth1 + fine_corr
    before2 = before1 + shifted_final[0]
    earlier2 = jnp.concatenate([before2[None], smooth2[:-1]], axis=0)
    smooth3 = smooth2 + damping * widened_smooth(smooth2, earlier2, source, cond_wide, inside_mask)
    before3 = fine_before(smooth3)
    resid3 = fine_residual(smooth3, before3, source, conduct)
    return (smooth3, resid3)


def solution(mesh):
    return jax.shard_map(
        shards,
        mesh=mesh,
        in_specs=(
            P("tm", "space", None),
            P("tm", "space", None),
            P("space", None),
            P("space", None),
        ),
        out_specs=(P("tm", "space", None), P("tm", "space", None)),
        check_vma=False,
    )
```

profile of v0, /device:TPU:100, one launch (start us, length us, event | category | flops | bytes accessed | tf_op | source)
XLA Modules:
  0.0 162.0 jit_solution(4502473798915692248)
XLA Ops:
  0.6 0.8 fusion.105
  1.4 1.9 %collective-permute-start.3 = (f32[2,1024]{1,0:T(2,128)S(1)}, f32[2,1024]{1,0:T(2,128)S(1)}, u32[]{:S(2)}, u32[]{:S(2)}) collective-permute-start(f32[2,1024]{1,0:T(2,128)S(1)} %get-tuple-element.44), channel_id=1, source_target_pairs={{0,1},{1,2},{2,3},{3,4},{4,5},{5,6},{6,7},{7,8},{8,9},{9,10},{10,1... | collective-permute-start | bytes 24584 | tf_op jit(solution)/shard_map/ppermute | solution.py:17
  3.3 5.8 %collective-permute-start.4 = (f32[2,1024]{1,0:T(2,128)S(1)}, f32[2,1024]{1,0:T(2,128)S(1)}, u32[]{:S(2)}, u32[]{:S(2)}) collective-permute-start(f32[2,1024]{1,0:T(2,128)S(1)} %get-tuple-element.45), channel_id=1, source_target_pairs={{1,0},{2,1},{3,2},{4,3},{5,4},{6,5},{7,6},{8,7},{9,8},{10,9},{11,1... | collective-permute-start | bytes 24584 | tf_op jit(solution)/shard_map/ppermute | solution.py:19
  9.1 1.0 slice_bitcast_fusion.17
  10.1 3.2 %collective-permute-start = (f32[64,1024]{1,0:T(8,128)S(1)}, f32[64,1024]{1,0:T(8,128)S(1)}, u32[]{:S(2)}, u32[]{:S(2)}) collective-permute-start(f32[64,1024]{1,0:T(8,128)S(1)} %slice_bitcast_fusion.17), channel_id=1, source_target_pairs={{0,32},{32,64},{64,96},{1,33},{33,65},{65,97},{2,34},{34,66},{66,9... | collective-permute-start | bytes 786440 | tf_op jit(solution)/shard_map/ppermute | solution.py:29
  13.3 1.0 broadcast_multiply_fusion.1
  14.5 4.0 %collective-permute-done = f32[64,1024]{1,0:T(8,128)S(1)} collective-permute-done((f32[64,1024]{1,0:T(8,128)S(1)}, f32[64,1024]{1,0:T(8,128)S(1)}, u32[]{:S(2)}, u32[]{:S(2)}) %collective-permute-start) | collective-permute-done | bytes 262176 | tf_op jit(solution)/shard_map/ppermute | solution.py:29
  18.8 1.3 copy-done
  20.1 0.6 copy-done.2
  20.7 1.1 pad_maximum_fusion.3
  22.0 1.9 %collective-permute-start.1 = (f32[3,8,2,1024]{3,2,1,0:T(2,128)S(1)}, f32[3,8,2,1024]{3,2,1,0:T(2,128)S(1)}, u32[]{:S(2)}, u32[]{:S(2)}) collective-permute-start(f32[3,8,2,1024]{3,2,1,0:T(2,128)S(1)} %get-tuple-element.18), channel_id=1, source_target_pairs={{0,1},{1,2},{2,3},{3,4},{4,5},{5,6},{6,7},{7,8},{8,9},{9,10},{10,1... | collective-permute-start | bytes 589832 | tf_op jit(solution)/shard_map/ppermute | solution.py:17
  24.0 5.8 %collective-permute-start.2 = (f32[3,8,2,1024]{3,2,1,0:T(2,128)S(1)}, f32[3,8,2,1024]{3,2,1,0:T(2,128)S(1)}, u32[]{:S(2)}, u32[]{:S(2)}) collective-permute-start(f32[3,8,2,1024]{3,2,1,0:T(2,128)S(1)} %get-tuple-element.19), channel_id=1, source_target_pairs={{1,0},{2,1},{3,2},{4,3},{5,4},{6,5},{7,6},{8,7},{9,8},{10,9},{11,1... | collective-permute-start | bytes 589832 | tf_op jit(solution)/shard_map/ppermute | solution.py:19
  29.8 1.3 collective-permute-done.1
  31.1 1.8 %collective-permute-done.2 = f32[3,8,2,1024]{3,2,1,0:T(2,128)S(1)} collective-permute-done((f32[3,8,2,1024]{3,2,1,0:T(2,128)S(1)}, f32[3,8,2,1024]{3,2,1,0:T(2,128)S(1)}, u32[]{:S(2)}, u32[]{:S(2)}) %collective-permute-start.2) | collective-permute-done | bytes 196640 | tf_op jit(solution)/shard_map/ppermute | solution.py:19
  32.9 1.7 %fusion.1 = f32[3,8,68,1024]{3,2,1,0:T(8,128)S(1)} fusion(f32[1,8,64,1024]{3,2,1,0:T(8,128)S(1)} %bitcast.74, f32[3,8,2,1024]{3,2,1,0:T(2,128)S(1)} %collective-permute-done.2, f32[1,8,64,1024]{3,2,1,0:T(8,128)S(1)} %maximum_bitcast_fusion, f32[1,8,64,1024]{3,2,1,0:T(8,128)S(1)} %bitcast.83, f32[3,8,2,1024]{3,2,1,0:T(2,128)S(1)} %collective-permute-done.1), kind=kLoop, calls=%fused_computation.5 | loop fusion | flops 6684672 | bytes 13369344 | tf_op jit(solution)/shard_map/concatenate | solution.py:15
  34.6 1.3 slice_bitcast_fusion.5
  35.9 2.5 %broadcast_divide_fusion.1 = (f32[8,66,1024]{2,1,0:T(8,128)S(1)}, f32[8,66,1024]{2,1,0:T(8,128)S(1)}) fusion(f32[66,1024]{1,0:T(8,128)S(1)} %get-tuple-element.39, f32[66]{0:T(128)S(1)} %and_convert_fusion, f32[8,68,1024]{2,1,0:T(8,128)S(1)} %get-tuple-element.14, f32[66,1024]{1,0:T(8,128)S(1)} %get-tuple-element.38, ...), kind=kLoop, calls=%fused_computation.137 | loop fusion | flops 5947392 | bytes 19071488 | tf_op jit(solution)/shard_map/div | solution.py:69
  38.5 2.2 %multiply_add_fusion.1 = f32[8,64,1024]{2,1,0:T(8,128)S(1)} fusion(f32[8,64,1024]{2,1,0:T(8,128)S(1)} %copy-done.2, f32[8,66,1024]{2,1,0:T(8,128)S(1)} %get-tuple-element.8, f32[8,66,1024]{2,1,0:T(8,128)S(1)} %get-tuple-element.9, f32[64,1024]{1,0:T(8,128)S(1)} %slice.492, f32[64,1024]{1,0:T(8,128)S(1)} %copy-done.3), kind=kLoop, calls=%fused_computation.98 | loop fusion | flops 6291456 | bytes 15466496 | tf_op jit(solution)/shard_map/add | solution.py:91
  40.7 1.9 %collective-permute-start.7 = (f32[8,1,1024]{2,1,0:T(1,128)S(1)}, f32[8,1,1024]{2,1,0:T(1,128)S(1)}, u32[]{:S(2)}, u32[]{:S(2)}) collective-permute-start(f32[8,1,1024]{2,1,0:T(1,128)S(1)} %get-tuple-element.32), channel_id=1, source_target_pairs={{0,1},{1,2},{2,3},{3,4},{4,5},{5,6},{6,7},{7,8},{8,9},{9,10},{10,1... | collective-permute-start | bytes 98312 | tf_op jit(solution)/shard_map/ppermute | solution.py:17
  42.6 5.9 %collective-permute-start.6 = (f32[8,1,1024]{2,1,0:T(1,128)S(1)}, f32[8,1,1024]{2,1,0:T(1,128)S(1)}, u32[]{:S(2)}, u32[]{:S(2)}) collective-permute-start(f32[8,1,1024]{2,1,0:T(1,128)S(1)} %get-tuple-element.33), channel_id=1, source_target_pairs={{1,0},{2,1},{3,2},{4,3},{5,4},{6,5},{7,6},{8,7},{9,8},{10,9},{11,1... | collective-permute-start | bytes 98312 | tf_op jit(solution)/shard_map/ppermute | solution.py:19
  48.7 3.1 %collective-permute-start.5 = (f32[64,1024]{1,0:T(8,128)S(1)}, f32[64,1024]{1,0:T(8,128)S(1)}, u32[]{:S(2)}, u32[]{:S(2)}) collective-permute-start(f32[64,1024]{1,0:T(8,128)S(1)} %slice_bitcast_fusion.16), channel_id=1, source_target_pairs={{0,32},{32,64},{64,96},{1,33},{33,65},{65,97},{2,34},{34,66},{66,9... | collective-permute-start | bytes 786440 | tf_op jit(solution)/shard_map/ppermute | solution.py:29
  51.8 1.0 select_maximum_fusion.2
  52.8 4.1 %collective-permute-done.5 = f32[64,1024]{1,0:T(8,128)S(1)} collective-permute-done((f32[64,1024]{1,0:T(8,128)S(1)}, f32[64,1024]{1,0:T(8,128)S(1)}, u32[]{:S(2)}, u32[]{:S(2)}) %collective-permute-start.5) | collective-permute-done | bytes 262176 | tf_op jit(solution)/shard_map/ppermute | solution.py:29
  57.0 1.8 %fusion.47 = f32[8,64,1024]{2,1,0:T(8,128)S(1)} fusion(f32[8,64,1024]{2,1,0:T(8,128)S(1)} %multiply_add_fusion.1, f32[8,66,1026]{2,1,0:T(8,128)S(1)} %select_maximum_fusion.2, f32[8,1,1024]{2,1,0:T(1,128)S(1)} %collective-permute-done.7, f32[8,1,1024]{2,1,0:T(1,128)S(1)} %collective-permute-done.6, f32[8,64,1024]{2,1,0:T(8,128)S(1)} %copy-done, ...), kind=kLoop, calls=%fused_computation.85 | loop fusion | flops 6291456 | bytes 12910592 | tf_op jit(solution)/shard_map/sub | solution.py:47
  59.1 1.9 %collective-permute-start.9 = (f32[4,1,1024]{2,1,0:T(1,128)S(1)}, f32[4,1,1024]{2,1,0:T(1,128)S(1)}, u32[]{:S(2)}, u32[]{:S(2)}) collective-permute-start(f32[4,1,1024]{2,1,0:T(1,128)S(1)} %get-tuple-element.34), channel_id=1, source_target_pairs={{0,1},{1,2},{2,3},{3,4},{4,5},{5,6},{6,7},{7,8},{8,9},{9,10},{10,1... | collective-permute-start | bytes 49160 | tf_op jit(solution)/shard_map/ppermute | solution.py:17
  61.0 5.8 %collective-permute-start.8 = (f32[4,1,1024]{2,1,0:T(1,128)S(1)}, f32[4,1,1024]{2,1,0:T(1,128)S(1)}, u32[]{:S(2)}, u32[]{:S(2)}) collective-permute-start(f32[4,1,1024]{2,1,0:T(1,128)S(1)} %get-tuple-element.35), channel_id=1, source_target_pairs={{1,0},{2,1},{3,2},{4,3},{5,4},{6,5},{7,6},{8,7},{9,8},{10,9},{11,1... | collective-permute-start | bytes 49160 | tf_op jit(solution)/shard_map/ppermute | solution.py:19
  66.8 1.4 collective-permute-done.8
  68.2 0.5 select_maximum_fusion.4
  68.7 0.9 fusion.89
  69.6 3.1 %collective-permute-start.10 = (f32[64,1024]{1,0:T(8,128)S(1)}, f32[64,1024]{1,0:T(8,128)S(1)}, u32[]{:S(2)}, u32[]{:S(2)}) collective-permute-start(f32[64,1024]{1,0:T(8,128)S(1)} %slice_bitcast_fusion.15), channel_id=1, source_target_pairs={{0,32},{32,64},{64,96},{1,33},{33,65},{65,97},{2,34},{34,66},{66,9... | collective-permute-start | bytes 786440 | tf_op jit(solution)/shard_map/ppermute | solution.py:29
  72.9 4.9 %collective-permute-done.10 = f32[64,1024]{1,0:T(8,128)S(1)} collective-permute-done((f32[64,1024]{1,0:T(8,128)S(1)}, f32[64,1024]{1,0:T(8,128)S(1)}, u32[]{:S(2)}, u32[]{:S(2)}) %collective-permute-start.10) | collective-permute-done | bytes 262176 | tf_op jit(solution)/shard_map/ppermute | solution.py:29
  78.4 1.9 %collective-permute-start.11 = (f32[3,4,2,1024]{3,2,1,0:T(2,128)S(1)}, f32[3,4,2,1024]{3,2,1,0:T(2,128)S(1)}, u32[]{:S(2)}, u32[]{:S(2)}) collective-permute-start(f32[3,4,2,1024]{3,2,1,0:T(2,128)S(1)} %get-tuple-element.28), channel_id=1, source_target_pairs={{0,1},{1,2},{2,3},{3,4},{4,5},{5,6},{6,7},{7,8},{8,9},{9,10},{10,1... | collective-permute-start | bytes 294920 | tf_op jit(solution)/shard_map/ppermute | solution.py:17
  80.4 5.9 %collective-permute-start.12 = (f32[3,4,2,1024]{3,2,1,0:T(2,128)S(1)}, f32[3,4,2,1024]{3,2,1,0:T(2,128)S(1)}, u32[]{:S(2)}, u32[]{:S(2)}) collective-permute-start(f32[3,4,2,1024]{3,2,1,0:T(2,128)S(1)} %get-tuple-element.29), channel_id=1, source_target_pairs={{1,0},{2,1},{3,2},{4,3},{5,4},{6,5},{7,6},{8,7},{9,8},{10,9},{11,1... | collective-permute-start | bytes 294920 | tf_op jit(solution)/shard_map/ppermute | solution.py:19
  86.5 1.8 %collective-permute-done.12 = f32[3,4,2,1024]{3,2,1,0:T(2,128)S(1)} collective-permute-done((f32[3,4,2,1024]{3,2,1,0:T(2,128)S(1)}, f32[3,4,2,1024]{3,2,1,0:T(2,128)S(1)}, u32[]{:S(2)}, u32[]{:S(2)}) %collective-permute-start.12) | collective-permute-done | bytes 98336 | tf_op jit(solution)/shard_map/ppermute | solution.py:19
  88.3 0.5 fusion.5
  88.8 0.4 slice_bitcast_fusion.11
  89.2 1.3 broadcast_divide_fusion.3
  90.4 1.0 multiply_add_fusion.3
  91.5 3.1 %collective-permute-start.13 = (f32[64,1024]{1,0:T(8,128)S(1)}, f32[64,1024]{1,0:T(8,128)S(1)}, u32[]{:S(2)}, u32[]{:S(2)}) collective-permute-start(f32[64,1024]{1,0:T(8,128)S(1)} %slice_bitcast_fusion.14), channel_id=1, source_target_pairs={{0,32},{32,64},{64,96},{1,33},{33,65},{65,97},{2,34},{34,66},{66,9... | collective-permute-start | bytes 786440 | tf_op jit(solution)/shard_map/ppermute | solution.py:29
  94.7 5.1 %collective-permute-done.13 = f32[64,1024]{1,0:T(8,128)S(1)} collective-permute-done((f32[64,1024]{1,0:T(8,128)S(1)}, f32[64,1024]{1,0:T(8,128)S(1)}, u32[]{:S(2)}, u32[]{:S(2)}) %collective-permute-start.13) | collective-permute-done | bytes 262176 | tf_op jit(solution)/shard_map/ppermute | solution.py:29
  100.3 1.9 %collective-permute-start.14 = (f32[3,4,2,1024]{3,2,1,0:T(2,128)S(1)}, f32[3,4,2,1024]{3,2,1,0:T(2,128)S(1)}, u32[]{:S(2)}, u32[]{:S(2)}) collective-permute-start(f32[3,4,2,1024]{3,2,1,0:T(2,128)S(1)} %get-tuple-element.26), channel_id=1, source_target_pairs={{0,1},{1,2},{2,3},{3,4},{4,5},{5,6},{6,7},{7,8},{8,9},{9,10},{10,1... | collective-permute-start | bytes 294920 | tf_op jit(solution)/shard_map/ppermute | solution.py:17
  102.2 5.8 %collective-permute-start.15 = (f32[3,4,2,1024]{3,2,1,0:T(2,128)S(1)}, f32[3,4,2,1024]{3,2,1,0:T(2,128)S(1)}, u32[]{:S(2)}, u32[]{:S(2)}) collective-permute-start(f32[3,4,2,1024]{3,2,1,0:T(2,128)S(1)} %get-tuple-element.27), channel_id=1, source_target_pairs={{1,0},{2,1},{3,2},{4,3},{5,4},{6,5},{7,6},{8,7},{9,8},{10,9},{11,1... | collective-permute-start | bytes 294920 | tf_op jit(solution)/shard_map/ppermute | solution.py:19
  108.3 1.8 %collective-permute-done.15 = f32[3,4,2,1024]{3,2,1,0:T(2,128)S(1)} collective-permute-done((f32[3,4,2,1024]{3,2,1,0:T(2,128)S(1)}, f32[3,4,2,1024]{3,2,1,0:T(2,128)S(1)}, u32[]{:S(2)}, u32[]{:S(2)}) %collective-permute-start.15) | collective-permute-done | bytes 98336 | tf_op jit(solution)/shard_map/ppermute | solution.py:19
  110.2 0.5 fusion.7
  111.0 1.3 broadcast_divide_fusion.2
  112.3 1.1 multiply_add_fusion.2
  113.3 3.1 %collective-permute-start.16 = (f32[64,1024]{1,0:T(8,128)S(1)}, f32[64,1024]{1,0:T(8,128)S(1)}, u32[]{:S(2)}, u32[]{:S(2)}) collective-permute-start(f32[64,1024]{1,0:T(8,128)S(1)} %slice_bitcast_fusion.13), channel_id=1, source_target_pairs={{0,32},{32,64},{64,96},{1,33},{33,65},{65,97},{2,34},{34,66},{66,9... | collective-permute-start | bytes 786440 | tf_op jit(solution)/shard_map/ppermute | solution.py:29
  116.5 5.1 %collective-permute-done.16 = f32[64,1024]{1,0:T(8,128)S(1)} collective-permute-done((f32[64,1024]{1,0:T(8,128)S(1)}, f32[64,1024]{1,0:T(8,128)S(1)}, u32[]{:S(2)}, u32[]{:S(2)}) %collective-permute-start.16) | collective-permute-done | bytes 262176 | tf_op jit(solution)/shard_map/ppermute | solution.py:29
  122.2 0.5 bitcast_add_fusion
  123.0 1.1 pad_maximum_fusion.2
  124.3 1.9 %collective-permute-start.17 = (f32[3,8,2,1024]{3,2,1,0:T(2,128)S(1)}, f32[3,8,2,1024]{3,2,1,0:T(2,128)S(1)}, u32[]{:S(2)}, u32[]{:S(2)}) collective-permute-start(f32[3,8,2,1024]{3,2,1,0:T(2,128)S(1)} %get-tuple-element.16), channel_id=1, source_target_pairs={{0,1},{1,2},{2,3},{3,4},{4,5},{5,6},{6,7},{7,8},{8,9},{9,10},{10,1... | collective-permute-start | bytes 589832 | tf_op jit(solution)/shard_map/ppermute | solution.py:17
  126.2 6.0 %collective-permute-start.18 = (f32[3,8,2,1024]{3,2,1,0:T(2,128)S(1)}, f32[3,8,2,1024]{3,2,1,0:T(2,128)S(1)}, u32[]{:S(2)}, u32[]{:S(2)}) collective-permute-start(f32[3,8,2,1024]{3,2,1,0:T(2,128)S(1)} %get-tuple-element.17), channel_id=1, source_target_pairs={{1,0},{2,1},{3,2},{4,3},{5,4},{6,5},{7,6},{8,7},{9,8},{10,9},{11,1... | collective-permute-start | bytes 589832 | tf_op jit(solution)/shard_map/ppermute | solution.py:19
  132.2 1.2 collective-permute-done.17
  133.4 1.8 %collective-permute-done.18 = f32[3,8,2,1024]{3,2,1,0:T(2,128)S(1)} collective-permute-done((f32[3,8,2,1024]{3,2,1,0:T(2,128)S(1)}, f32[3,8,2,1024]{3,2,1,0:T(2,128)S(1)}, u32[]{:S(2)}, u32[]{:S(2)}) %collective-permute-start.18) | collective-permute-done | bytes 196640 | tf_op jit(solution)/shard_map/ppermute | solution.py:19
  135.1 1.7 %fusion.3 = f32[3,8,68,1024]{3,2,1,0:T(8,128)S(1)} fusion(f32[1,8,64,1024]{3,2,1,0:T(8,128)S(1)} %bitcast.76, f32[3,8,2,1024]{3,2,1,0:T(2,128)S(1)} %collective-permute-done.18, f32[1,8,64,1024]{3,2,1,0:T(8,128)S(1)} %maximum_bitcast_fusion.1, f32[1,8,64,1024]{3,2,1,0:T(8,128)S(1)} %bitcast.78, f32[3,8,2,1024]{3,2,1,0:T(2,128)S(1)} %collective-permute-done.17), kind=kLoop, calls=%fused_computation.7 | loop fusion | flops 6684672 | bytes 13369344 | tf_op jit(solution)/shard_map/concatenate | solution.py:15
  136.9 1.3 slice_bitcast_fusion.2
  138.2 2.5 %broadcast_divide_fusion = (f32[8,66,1024]{2,1,0:T(8,128)S(1)}, f32[8,66,1024]{2,1,0:T(8,128)S(1)}) fusion(f32[66,1024]{1,0:T(8,128)S(1)} %get-tuple-element.39, f32[66]{0:T(128)S(1)} %and_convert_fusion, f32[8,68,1024]{2,1,0:T(8,128)S(1)} %get-tuple-element.11, f32[66,1024]{1,0:T(8,128)S(1)} %get-tuple-element.38, ...), kind=kLoop, calls=%fused_computation.136 | loop fusion | flops 5947392 | bytes 19071488 | tf_op jit(solution)/shard_map/div | solution.py:69
  140.7 2.2 %multiply_add_fusion = f32[8,64,1024]{2,1,0:T(8,128)S(1)} fusion(f32[8,64,1024]{2,1,0:T(8,128)S(1)} %bitcast_add_fusion, f32[8,66,1024]{2,1,0:T(8,128)S(1)} %get-tuple-element.2, f32[8,66,1024]{2,1,0:T(8,128)S(1)} %get-tuple-element.3, f32[64,1024]{1,0:T(8,128)S(1)} %slice.492, f32[64,1024]{1,0:T(8,128)S(1)} %copy-done.3), kind=kLoop, calls=%fused_computation.97 | loop fusion | flops 6291456 | bytes 15466496 | tf_op jit(solution)/shard_map/add | solution.py:108
  142.9 1.9 %collective-permute-start.21 = (f32[8,1,1024]{2,1,0:T(1,128)S(1)}, f32[8,1,1024]{2,1,0:T(1,128)S(1)}, u32[]{:S(2)}, u32[]{:S(2)}) collective-permute-start(f32[8,1,1024]{2,1,0:T(1,128)S(1)} %get-tuple-element.30), channel_id=1, source_target_pairs={{0,1},{1,2},{2,3},{3,4},{4,5},{5,6},{6,7},{7,8},{8,9},{9,10},{10,1... | collective-permute-start | bytes 98312 | tf_op jit(solution)/shard_map/ppermute | solution.py:17
  144.9 5.9 %collective-permute-start.20 = (f32[8,1,1024]{2,1,0:T(1,128)S(1)}, f32[8,1,1024]{2,1,0:T(1,128)S(1)}, u32[]{:S(2)}, u32[]{:S(2)}) collective-permute-start(f32[8,1,1024]{2,1,0:T(1,128)S(1)} %get-tuple-element.31), channel_id=1, source_target_pairs={{1,0},{2,1},{3,2},{4,3},{5,4},{6,5},{7,6},{8,7},{9,8},{10,9},{11,1... | collective-permute-start | bytes 98312 | tf_op jit(solution)/shard_map/ppermute | solution.py:19
  151.0 3.1 %collective-permute-start.19 = (f32[64,1024]{1,0:T(8,128)S(1)}, f32[64,1024]{1,0:T(8,128)S(1)}, u32[]{:S(2)}, u32[]{:S(2)}) collective-permute-start(f32[64,1024]{1,0:T(8,128)S(1)} %slice_bitcast_fusion.12), channel_id=1, source_target_pairs={{0,32},{32,64},{64,96},{1,33},{33,65},{65,97},{2,34},{34,66},{66,9... | collective-permute-start | bytes 786440 | tf_op jit(solution)/shard_map/ppermute | solution.py:29
  154.1 1.0 select_maximum_fusion
  155.1 4.1 %collective-permute-done.19 = f32[64,1024]{1,0:T(8,128)S(1)} collective-permute-done((f32[64,1024]{1,0:T(8,128)S(1)}, f32[64,1024]{1,0:T(8,128)S(1)}, u32[]{:S(2)}, u32[]{:S(2)}) %collective-permute-start.19) | collective-permute-done | bytes 262176 | tf_op jit(solution)/shard_map/ppermute | solution.py:29
  159.3 2.7 %fusion.42 = f32[8,64,1024]{2,1,0:T(8,128)} fusion(f32[8,64,1024]{2,1,0:T(8,128)S(1)} %multiply_add_fusion, f32[8,66,1026]{2,1,0:T(8,128)S(1)} %select_maximum_fusion, f32[8,1,1024]{2,1,0:T(1,128)S(1)} %collective-permute-done.21, f32[8,1,1024]{2,1,0:T(1,128)S(1)} %collective-permute-done.20, f32[8,64,1024]{2,1,0:T(8,128)S(1)} %copy-done, ...), kind=kLoop, calls=%fused_computation.75 | loop fusion | flops 6291456 | bytes 12910592 | tf_op jit(solution)/shard_map/sub | solution.py:47
  (60 shorter events, 4.6 us)
Async XLA Ops:
  1.4 13.0 %collective-permute-start.3 = (f32[2,1024]{1,0:T(2,128)S(1)}, f32[2,1024]{1,0:T(2,128)S(1)}, u32[]{:S(2)}, u32[]{:S(2)}) collective-permute-start(f32[2,1024]{1,0:T(2,128)S(1)} %get-tuple-element.44), channel_id=1, source_target_pairs={{0,1},{1,2},{2,3},{3,4},{4,5},{5,6},{6,7},{7,8},{8,9},{9,10},{10,1... | collective-permute-start | bytes 24584 | tf_op jit(solution)/shard_map/ppermute | solution.py:17
  3.3 11.1 %collective-permute-start.4 = (f32[2,1024]{1,0:T(2,128)S(1)}, f32[2,1024]{1,0:T(2,128)S(1)}, u32[]{:S(2)}, u32[]{:S(2)}) collective-permute-start(f32[2,1024]{1,0:T(2,128)S(1)} %get-tuple-element.45), channel_id=1, source_target_pairs={{1,0},{2,1},{3,2},{4,3},{5,4},{6,5},{7,6},{8,7},{9,8},{10,9},{11,1... | collective-permute-start | bytes 24584 | tf_op jit(solution)/shard_map/ppermute | solution.py:19
  10.1 4.3 %copy-start.3 = (f32[64,1024]{1,0:T(8,128)S(1)}, f32[64,1024]{1,0:T(8,128)}, u32[]{:S(2)}) copy-start(f32[64,1024]{1,0:T(8,128)} %param.7) | copy-start | bytes 786436
  10.1 8.4 %collective-permute-start = (f32[64,1024]{1,0:T(8,128)S(1)}, f32[64,1024]{1,0:T(8,128)S(1)}, u32[]{:S(2)}, u32[]{:S(2)}) collective-permute-start(f32[64,1024]{1,0:T(8,128)S(1)} %slice_bitcast_fusion.17), channel_id=1, source_target_pairs={{0,32},{32,64},{64,96},{1,33},{33,65},{65,97},{2,34},{34,66},{66,9... | collective-permute-start | bytes 786440 | tf_op jit(solution)/shard_map/ppermute | solution.py:29
  14.3 4.1 %copy-start.4 = (f32[64,1024]{1,0:T(8,128)S(1)}, f32[64,1024]{1,0:T(8,128)}, u32[]{:S(2)}) copy-start(f32[64,1024]{1,0:T(8,128)} %param.6) | copy-start | bytes 786436
  14.4 4.2 %slice-start = ((f32[8,64,1024]{2,1,0:T(8,128)}), f32[7,64,1024]{2,1,0:T(8,128)S(1)}, s32[]{:S(2)}) async-start(f32[8,64,1024]{2,1,0:T(8,128)} %param.5), calls=%async_computation | async-start | bytes 3670016 | tf_op jit(solution)/shard_map/slice | solution.py:90
  18.5 1.6 copy-start
  18.5 2.2 %copy-start.2 = (f32[8,64,1024]{2,1,0:T(8,128)S(1)}, f32[8,64,1024]{2,1,0:T(8,128)}, u32[]{:S(2)}) copy-start(f32[8,64,1024]{2,1,0:T(8,128)} %param.5) | copy-start | bytes 6291460
  22.0 9.1 %collective-permute-start.1 = (f32[3,8,2,1024]{3,2,1,0:T(2,128)S(1)}, f32[3,8,2,1024]{3,2,1,0:T(2,128)S(1)}, u32[]{:S(2)}, u32[]{:S(2)}) collective-permute-start(f32[3,8,2,1024]{3,2,1,0:T(2,128)S(1)} %get-tuple-element.18), channel_id=1, source_target_pairs={{0,1},{1,2},{2,3},{3,4},{4,5},{5,6},{6,7},{7,8},{8,9},{9,10},{10,1... | collective-permute-start | bytes 589832 | tf_op jit(solution)/shard_map/ppermute | solution.py:17
  24.0 8.9 %collective-permute-start.2 = (f32[3,8,2,1024]{3,2,1,0:T(2,128)S(1)}, f32[3,8,2,1024]{3,2,1,0:T(2,128)S(1)}, u32[]{:S(2)}, u32[]{:S(2)}) collective-permute-start(f32[3,8,2,1024]{3,2,1,0:T(2,128)S(1)} %get-tuple-element.19), channel_id=1, source_target_pairs={{1,0},{2,1},{3,2},{4,3},{5,4},{6,5},{7,6},{8,7},{9,8},{10,9},{11,1... | collective-permute-start | bytes 589832 | tf_op jit(solution)/shard_map/ppermute | solution.py:19
  40.7 11.1 %collective-permute-start.7 = (f32[8,1,1024]{2,1,0:T(1,128)S(1)}, f32[8,1,1024]{2,1,0:T(1,128)S(1)}, u32[]{:S(2)}, u32[]{:S(2)}) collective-permute-start(f32[8,1,1024]{2,1,0:T(1,128)S(1)} %get-tuple-element.32), channel_id=1, source_target_pairs={{0,1},{1,2},{2,3},{3,4},{4,5},{5,6},{6,7},{7,8},{8,9},{9,10},{10,1... | collective-permute-start | bytes 98312 | tf_op jit(solution)/shard_map/ppermute | solution.py:17
  42.6 9.2 %collective-permute-start.6 = (f32[8,1,1024]{2,1,0:T(1,128)S(1)}, f32[8,1,1024]{2,1,0:T(1,128)S(1)}, u32[]{:S(2)}, u32[]{:S(2)}) collective-permute-start(f32[8,1,1024]{2,1,0:T(1,128)S(1)} %get-tuple-element.33), channel_id=1, source_target_pairs={{1,0},{2,1},{3,2},{4,3},{5,4},{6,5},{7,6},{8,7},{9,8},{10,9},{11,1... | collective-permute-start | bytes 98312 | tf_op jit(solution)/shard_map/ppermute | solution.py:19
  48.7 8.3 %collective-permute-start.5 = (f32[64,1024]{1,0:T(8,128)S(1)}, f32[64,1024]{1,0:T(8,128)S(1)}, u32[]{:S(2)}, u32[]{:S(2)}) collective-permute-start(f32[64,1024]{1,0:T(8,128)S(1)} %slice_bitcast_fusion.16), channel_id=1, source_target_pairs={{0,32},{32,64},{64,96},{1,33},{33,65},{65,97},{2,34},{34,66},{66,9... | collective-permute-start | bytes 786440 | tf_op jit(solution)/shard_map/ppermute | solution.py:29
  59.1 7.7 %collective-permute-start.9 = (f32[4,1,1024]{2,1,0:T(1,128)S(1)}, f32[4,1,1024]{2,1,0:T(1,128)S(1)}, u32[]{:S(2)}, u32[]{:S(2)}) collective-permute-start(f32[4,1,1024]{2,1,0:T(1,128)S(1)} %get-tuple-element.34), channel_id=1, source_target_pairs={{0,1},{1,2},{2,3},{3,4},{4,5},{5,6},{6,7},{7,8},{8,9},{9,10},{10,1... | collective-permute-start | bytes 49160 | tf_op jit(solution)/shard_map/ppermute | solution.py:17
  61.0 7.2 %collective-permute-start.8 = (f32[4,1,1024]{2,1,0:T(1,128)S(1)}, f32[4,1,1024]{2,1,0:T(1,128)S(1)}, u32[]{:S(2)}, u32[]{:S(2)}) collective-permute-start(f32[4,1,1024]{2,1,0:T(1,128)S(1)} %get-tuple-element.35), channel_id=1, source_target_pairs={{1,0},{2,1},{3,2},{4,3},{5,4},{6,5},{7,6},{8,7},{9,8},{10,9},{11,1... | collective-permute-start | bytes 49160 | tf_op jit(solution)/shard_map/ppermute | solution.py:19
  69.6 8.3 %collective-permute-start.10 = (f32[64,1024]{1,0:T(8,128)S(1)}, f32[64,1024]{1,0:T(8,128)S(1)}, u32[]{:S(2)}, u32[]{:S(2)}) collective-permute-start(f32[64,1024]{1,0:T(8,128)S(1)} %slice_bitcast_fusion.15), channel_id=1, source_target_pairs={{0,32},{32,64},{64,96},{1,33},{33,65},{65,97},{2,34},{34,66},{66,9... | collective-permute-start | bytes 786440 | tf_op jit(solution)/shard_map/ppermute | solution.py:29
  78.4 8.0 %collective-permute-start.11 = (f32[3,4,2,1024]{3,2,1,0:T(2,128)S(1)}, f32[3,4,2,1024]{3,2,1,0:T(2,128)S(1)}, u32[]{:S(2)}, u32[]{:S(2)}) collective-permute-start(f32[3,4,2,1024]{3,2,1,0:T(2,128)S(1)} %get-tuple-element.28), channel_id=1, source_target_pairs={{0,1},{1,2},{2,3},{3,4},{4,5},{5,6},{6,7},{7,8},{8,9},{9,10},{10,1... | collective-permute-start | bytes 294920 | tf_op jit(solution)/shard_map/ppermute | solution.py:17
  80.4 8.0 %collective-permute-start.12 = (f32[3,4,2,1024]{3,2,1,0:T(2,128)S(1)}, f32[3,4,2,1024]{3,2,1,0:T(2,128)S(1)}, u32[]{:S(2)}, u32[]{:S(2)}) collective-permute-start(f32[3,4,2,1024]{3,2,1,0:T(2,128)S(1)} %get-tuple-element.29), channel_id=1, source_target_pairs={{1,0},{2,1},{3,2},{4,3},{5,4},{6,5},{7,6},{8,7},{9,8},{10,9},{11,1... | collective-permute-start | bytes 294920 | tf_op jit(solution)/shard_map/ppermute | solution.py:19
  91.5 8.3 %collective-permute-start.13 = (f32[64,1024]{1,0:T(8,128)S(1)}, f32[64,1024]{1,0:T(8,128)S(1)}, u32[]{:S(2)}, u32[]{:S(2)}) collective-permute-start(f32[64,1024]{1,0:T(8,128)S(1)} %slice_bitcast_fusion.14), channel_id=1, source_target_pairs={{0,32},{32,64},{64,96},{1,33},{33,65},{65,97},{2,34},{34,66},{66,9... | collective-permute-start | bytes 786440 | tf_op jit(solution)/shard_map/ppermute | solution.py:29
  100.3 8.0 %collective-permute-start.14 = (f32[3,4,2,1024]{3,2,1,0:T(2,128)S(1)}, f32[3,4,2,1024]{3,2,1,0:T(2,128)S(1)}, u32[]{:S(2)}, u32[]{:S(2)}) collective-permute-start(f32[3,4,2,1024]{3,2,1,0:T(2,128)S(1)} %get-tuple-element.26), channel_id=1, source_target_pairs={{0,1},{1,2},{2,3},{3,4},{4,5},{5,6},{6,7},{7,8},{8,9},{9,10},{10,1... | collective-permute-start | bytes 294920 | tf_op jit(solution)/shard_map/ppermute | solution.py:17
  102.2 8.0 %collective-permute-start.15 = (f32[3,4,2,1024]{3,2,1,0:T(2,128)S(1)}, f32[3,4,2,1024]{3,2,1,0:T(2,128)S(1)}, u32[]{:S(2)}, u32[]{:S(2)}) collective-permute-start(f32[3,4,2,1024]{3,2,1,0:T(2,128)S(1)} %get-tuple-element.27), channel_id=1, source_target_pairs={{1,0},{2,1},{3,2},{4,3},{5,4},{6,5},{7,6},{8,7},{9,8},{10,9},{11,1... | collective-permute-start | bytes 294920 | tf_op jit(solution)/shard_map/ppermute | solution.py:19
  113.3 8.3 %collective-permute-start.16 = (f32[64,1024]{1,0:T(8,128)S(1)}, f32[64,1024]{1,0:T(8,128)S(1)}, u32[]{:S(2)}, u32[]{:S(2)}) collective-permute-start(f32[64,1024]{1,0:T(8,128)S(1)} %slice_bitcast_fusion.13), channel_id=1, source_target_pairs={{0,32},{32,64},{64,96},{1,33},{33,65},{65,97},{2,34},{34,66},{66,9... | collective-permute-start | bytes 786440 | tf_op jit(solution)/shard_map/ppermute | solution.py:29
  124.3 9.1 %collective-permute-start.17 = (f32[3,8,2,1024]{3,2,1,0:T(2,128)S(1)}, f32[3,8,2,1024]{3,2,1,0:T(2,128)S(1)}, u32[]{:S(2)}, u32[]{:S(2)}) collective-permute-start(f32[3,8,2,1024]{3,2,1,0:T(2,128)S(1)} %get-tuple-element.16), channel_id=1, source_target_pairs={{0,1},{1,2},{2,3},{3,4},{4,5},{5,6},{6,7},{7,8},{8,9},{9,10},{10,1... | collective-permute-start | bytes 589832 | tf_op jit(solution)/shard_map/ppermute | solution.py:17
  126.2 8.9 %collective-permute-start.18 = (f32[3,8,2,1024]{3,2,1,0:T(2,128)S(1)}, f32[3,8,2,1024]{3,2,1,0:T(2,128)S(1)}, u32[]{:S(2)}, u32[]{:S(2)}) collective-permute-start(f32[3,8,2,1024]{3,2,1,0:T(2,128)S(1)} %get-tuple-element.17), channel_id=1, source_target_pairs={{1,0},{2,1},{3,2},{4,3},{5,4},{6,5},{7,6},{8,7},{9,8},{10,9},{11,1... | collective-permute-start | bytes 589832 | tf_op jit(solution)/shard_map/ppermute | solution.py:19
  142.9 16.4 %copy-start.1 = (f32[8,64,1024]{2,1,0:T(8,128)}, f32[8,64,1024]{2,1,0:T(8,128)S(1)}, u32[]{:S(2)}) copy-start(f32[8,64,1024]{2,1,0:T(8,128)S(1)} %multiply_add_fusion) | copy-start | bytes 6291460
  142.9 11.1 %collective-permute-start.21 = (f32[8,1,1024]{2,1,0:T(1,128)S(1)}, f32[8,1,1024]{2,1,0:T(1,128)S(1)}, u32[]{:S(2)}, u32[]{:S(2)}) collective-permute-start(f32[8,1,1024]{2,1,0:T(1,128)S(1)} %get-tuple-element.30), channel_id=1, source_target_pairs={{0,1},{1,2},{2,3},{3,4},{4,5},{5,6},{6,7},{7,8},{8,9},{9,10},{10,1... | collective-permute-start | bytes 98312 | tf_op jit(solution)/shard_map/ppermute | solution.py:17
  144.9 9.2 %collective-permute-start.20 = (f32[8,1,1024]{2,1,0:T(1,128)S(1)}, f32[8,1,1024]{2,1,0:T(1,128)S(1)}, u32[]{:S(2)}, u32[]{:S(2)}) collective-permute-start(f32[8,1,1024]{2,1,0:T(1,128)S(1)} %get-tuple-element.31), channel_id=1, source_target_pairs={{1,0},{2,1},{3,2},{4,3},{5,4},{6,5},{7,6},{8,7},{9,8},{10,9},{11,1... | collective-permute-start | bytes 98312 | tf_op jit(solution)/shard_map/ppermute | solution.py:19
  151.0 8.3 %collective-permute-start.19 = (f32[64,1024]{1,0:T(8,128)S(1)}, f32[64,1024]{1,0:T(8,128)S(1)}, u32[]{:S(2)}, u32[]{:S(2)}) collective-permute-start(f32[64,1024]{1,0:T(8,128)S(1)} %slice_bitcast_fusion.12), channel_id=1, source_target_pairs={{0,32},{32,64},{64,96},{1,33},{33,65},{65,97},{2,34},{34,66},{66,9... | collective-permute-start | bytes 786440 | tf_op jit(solution)/shard_map/ppermute | solution.py:29
where the time goes:
time: 163 us; the launch traced here: 162 us
  starting transfers between devices  80.9 us (50%)
  waiting for transfers between devices  38.9 us (24%)
  other arithmetic  32.4 us (20%)
  local copies, waits for them, and re-layouts  8.51 us (5%)
    ppermute x8, starting transfers between devices, extended(): lax.ppermute(head, axis, [((i + 1) % count, i) for i in range(ends)])  46.8 us
    ppermute x6, waiting for transfers between devices, passed_along(): return lax.ppermute(block, axis, route)  27.3 us
    ppermute x6, starting transfers between devices, passed_along(): return lax.ppermute(block, axis, route)  18.8 us
    ppermute x8, starting transfers between devices, extended(): lax.ppermute(tail, axis, [(i, (i + 1) % count) for i in range(ends)])  15.4 us
    ppermute x8, waiting for transfers between devices, extended(): lax.ppermute(head, axis, [((i + 1) % count, i) for i in range(ends)])  8.6 us
    div x4, other arithmetic, widened_smooth(): first_sweep = resid_wide / diagonal  7.53 us
    concatenate x7, other arithmetic, extended(): jnp.concatenate([lax.ppermute(tail, axis, [(i, (i + 1) % count) for i in...  6.93 us
    sub x2, other arithmetic, fine_residual(): return source + earlier - apply_operator(field, conduct)  4.54 us
  transfers between devices with their start and end apart: 22, of which 15 were waited for; matrix products, arithmetic and copies ran while one was open for 3% of the time, Pallas kernels for 0%

commit v1 on v0

v1 whole, which is shorter than its diff:
```python
import functools

import jax
import jax.numpy as jnp
from jax import lax
from jax.experimental import pallas as pl
from jax.experimental.pallas import tpu as pltpu
from jax.sharding import PartitionSpec as P

damping = 0.8
MESH = pl.DeviceIdType.MESH
LANES = 128
HALO = 8
TOP = 16
CHUNK = 16


def cycle_kernel(
    steps,
    rows,
    blocks,
    source_hbm,
    guess_hbm,
    start_hbm,
    cond_hbm,
    u3,
    res,
    src,
    gue,
    u1,
    u2,
    e0,
    e1,
    e2,
    rhs,
    tmp,
    coef,
    load_sem,
    xs,
    xr,
    hs,
    hr,
):
    half = steps // 2
    end = TOP + rows
    tm, sp = lax.axis_index("tm"), lax.axis_index("space")
    n_tm, n_sp = lax.axis_size("tm"), lax.axis_size("space")
    first, last = tm == 0, tm == n_tm - 1
    top, bottom = sp == 0, sp == n_sp - 1
    COND, INV, W, INVK, WK = range(5)

    def load(group, hbm, lead, buf, at, count):
        out = []
        for k in range(blocks):
            cols = pl.ds(k * LANES, LANES)
            view = hbm.at[:, cols] if lead is None else hbm.at[pl.ds(lead, count), :, cols]
            dst = buf.at[at, k, pl.ds(TOP, rows), :] if lead is None else buf.at[pl.ds(at, count), k, pl.ds(TOP, rows), :]
            out.append(pltpu.make_async_copy(view, dst, load_sem.at[group, k]))
        return out

    loads = {
        "g_last": load(0, guess_hbm, steps - 2, gue, steps - 1, 2),
        "cond": load(1, cond_hbm, None, coef, COND, 1),
        "s_last": load(2, source_hbm, steps - 2, src, steps - 2, 2),
        "g_rest": load(3, guess_hbm, 0, gue, 1, steps - 2),
        "s_rest": load(4, source_hbm, 0, src, 0, steps - 2),
    }
    starts = [load(5 + i, start_hbm, None, buf, 0, 1) for i, buf in enumerate((gue, u1, u3))]

    def start(copies):
        for c in copies:
            c.start()

    def wait(copies):
        for c in copies:
            c.wait()

    for name in ("g_last", "cond", "s_last", "g_rest", "s_rest"):
        start(loads[name])

    @pl.when(first)
    def _():
        for copies in starts:
            start(copies)

    barrier = pltpu.get_barrier_semaphore()

    def greet(cond, axis, index):
        @pl.when(cond)
        def _():
            pl.semaphore_signal(barrier, inc=1, device_id={axis: index}, device_id_type=MESH)

    greet(~first, "tm", tm - 1)
    greet(~last, "tm", tm + 1)
    greet(~top, "space", sp - 1)
    greet(~bottom, "space", sp + 1)
    one = jnp.int32(1)
    zero = jnp.int32(0)
    peers = (
        jnp.where(first, zero, one)
        + jnp.where(last, zero, one)
        + jnp.where(top, zero, one)
        + jnp.where(bottom, zero, one)
    )
    pl.semaphore_wait(barrier, peers)

    own = pl.ds(TOP, rows)

    def x_copy(i, buf, plane):
        return pltpu.make_async_remote_copy(
            src_ref=buf.at[plane, :, own, :],
            dst_ref=buf.at[0, :, own, :],
            send_sem=xs.at[i],
            recv_sem=xr.at[i],
            device_id={"tm": tm + 1},
            device_id_type=MESH,
        )

    x_plan = [(gue, steps), (u1, steps), (e0, half), (e1, half), (e2, half), (u3, steps)]

    def x_send(i):
        @pl.when(~last)
        def _():
            x_copy(i, *x_plan[i]).start()

    def x_wait(i):
        @pl.when(~first)
        def _():
            x_copy(i, *x_plan[i]).wait_recv()

        if i in (0, 1, 5):

            @pl.when(first)
            def _():
                wait(starts[(0, 1, 5).index(i)])

    h_plan = [
        (gue, steps - 1, 2),
        (src, steps - 2, 2),
        (coef, COND, 1),
        (gue, 1, steps - 2),
        (src, 0, steps - 2),
        (gue, 0, 1),
        (u1, 0, 1),
        (e0, 0, 1),
        (e1, 0, 1),
        (e2, 0, 1),
        (e2, half - 1, 2),
        (e2, 2, half - 3),
        (e2, 1, 1),
    ]

    def down_copy(i):
        buf, plane, count = h_plan[i]
        return pltpu.make_async_remote_copy(
            src_ref=buf.at[pl.ds(plane, count), :, pl.ds(end - HALO, HALO), :],
            dst_ref=buf.at[pl.ds(plane, count), :, pl.ds(TOP - HALO, HALO), :],
            send_sem=hs.at[i, 0],
            recv_sem=hr.at[i, 0],
            device_id={"space": sp + 1},
            device_id_type=MESH,
        )

    def up_copy(i):
        buf, plane, count = h_plan[i]
        return pltpu.make_async_remote_copy(
            src_ref=buf.at[pl.ds(plane, count), :, pl.ds(TOP, HALO), :],
            dst_ref=buf.at[pl.ds(plane, count), :, pl.ds(end, HALO), :],
            send_sem=hs.at[i, 1],
            recv_sem=hr.at[i, 1],
            device_id={"space": sp - 1},
            device_id_type=MESH,
        )

    def h_send(*which):
        @pl.when(~bottom)
        def _():
            for i in which:
                down_copy(i).start()

        @pl.when(~top)
        def _():
            for i in which:
                up_copy(i).start()

    def h_wait(*which):
        @pl.when(~top)
        def _():
            for i in which:
                down_copy(i).wait_recv()

        @pl.when(~bottom)
        def _():
            for i in which:
                up_copy(i).wait_recv()

    def at(buf, n, r):
        return buf[n, :, pl.ds(r, CHUNK), :]

    def put(buf, n, r, value):
        buf[n, :, pl.ds(r, CHUNK), :] = value

    def sideways(v):
        lane = lax.broadcasted_iota(jnp.int32, v.shape, 2)
        edge = jnp.zeros((1,) + v.shape[1:], jnp.float32)
        fwd = pltpu.roll(v, 1, 2)
        bwd = pltpu.roll(v, LANES - 1, 2)
        left = jnp.where(lane == 0, jnp.concatenate([edge, fwd[:-1]], axis=0), fwd)
        right = jnp.where(lane == LANES - 1, jnp.concatenate([bwd[1:], edge], axis=0), bwd)
        return left + right

    def with_sum(buf, n, r):
        v = at(buf, n, r)
        return v, (at(buf, n, r - 1) + at(buf, n, r + 1)) + sideways(v)

    def over_rows(low, high, body):
        count = (high - low) // CHUNK

        def step(i, carry):
            body(low + i * CHUNK)
            return carry

        lax.fori_loop(0, count, step, 0, unroll=True)

    def over_planes(low, high, body):
        if high - low == 1:
            body(low)
        else:

            def step(i, carry):
                body(i)
                return carry

            lax.fori_loop(low, high, step, 0)

    wide = (TOP - HALO, end + HALO)

    def fine_smooth(frm, to, low, high):
        def first_pass(n):
            def chunk(r):
                v, s = with_sum(frm, n + 1, r)
                rest = at(src, n, r) + at(frm, n, r)
                put(tmp, n, r, damping * (at(coef, INV, r) * rest + at(coef, W, r) * s - v))

            over_rows(*wide, chunk)

        def second_pass(n):
            def chunk(r):
                v, s = with_sum(tmp, n, r)
                put(to, n + 1, r, at(frm, n + 1, r) + (v + at(coef, W, r) * s))

            over_rows(*wide, chunk)

        over_planes(low, high, first_pass)
        over_planes(low, high, second_pass)

    def restrict(m):
        def chunk(r):
            a, sa = at(u1, 2 * m + 1, r), at(u1, 2 * m + 1, r - 1) + at(u1, 2 * m + 1, r + 1)
            b, sb = at(u1, 2 * m + 2, r), at(u1, 2 * m + 2, r - 1) + at(u1, 2 * m + 2, r + 1)
            pair = a + b
            around = (sa + sb) + sideways(pair)
            total = at(src, 2 * m, r) + at(src, 2 * m + 1, r) + (at(u1, 2 * m, r) - b)
            total = total - at(coef, COND, r) * (4.0 * pair - around)
            put(rhs, m, r, at(coef, INVK, r) * total)

        over_rows(*wide, chunk)

    def coarse_first(m):
        def chunk(r):
            v, s = with_sum(rhs, m, r)
            put(e0, m + 1, r, damping * (v + at(coef, WK, r) * s))

        over_rows(*wide, chunk)

    def coarse_sweep(frm, to, m, slot):
        def first_pass(r):
            v, s = with_sum(frm, m + 1, r)
            rest = at(rhs, m, r) + at(coef, INVK, r) * at(frm, m, r)
            put(tmp, slot, r, damping * (rest + at(coef, WK, r) * s - v))

        def second_pass(r):
            v, s = with_sum(tmp, slot, r)
            put(to, m + 1, r, at(frm, m + 1, r) + (v + at(coef, WK, r) * s))

        over_rows(*wide, first_pass)
        over_rows(*((TOP, end) if to is e2 else wide), second_pass)

    def prolong_odd(m):
        over_rows(*wide, lambda r: put(u2, 2 * m + 2, r, at(u1, 2 * m + 2, r) + at(e2, m + 1, r)))

    def prolong_even(m):
        over_rows(
            *wide,
            lambda r: put(u2, 2 * m + 1, r, at(u1, 2 * m + 1, r) + 0.5 * (at(e2, m, r) + at(e2, m + 1, r))),
        )

    def last_residual(n):
        def chunk(r):
            v, s = with_sum(u3, n + 1, r)
            rest = at(src, n, r) + (at(u3, n, r) - v)
            res[n, :, pl.ds(r - TOP, CHUNK), :] = rest - at(coef, COND, r) * (4.0 * v - s)

        over_rows(TOP, end, chunk)

    def clear(low):
        zeros = jnp.zeros((blocks, HALO, LANES), jnp.float32)

        def planes(buf, a, b):
            for n in range(a, b):
                buf[n, :, pl.ds(low, HALO), :] = zeros

        planes(gue, 0, steps + 1)
        planes(src, 0, steps)
        planes(coef, COND, COND + 1)
        for buf in (u1, e0, e1):
            planes(buf, 0, 1)
        planes(e2, 0, half + 1)

    @pl.when(top)
    def _():
        clear(TOP - HALO)

    @pl.when(bottom)
    def _():
        clear(end)

    @pl.when(first)
    def _():
        for buf in (e0, e1, e2):
            buf[0, :, pl.ds(TOP, rows), :] = jnp.zeros((blocks, rows, LANES), jnp.float32)

    wait(loads["g_last"])
    x_send(0)
    h_send(0)
    wait(loads["cond"])
    wait(loads["s_last"])
    h_send(2, 1)
    wait(loads["g_rest"])
    wait(loads["s_rest"])
    h_send(3, 4)

    h_wait(2)

    def coefficients(r):
        c = at(coef, COND, r)
        inv = 1.0 / (1.0 + 4.0 * c)
        invk = 1.0 / (1.0 + 8.0 * c)
        put(coef, INV, r, inv)
        put(coef, W, r, c * inv)
        put(coef, INVK, r, invk)
        put(coef, WK, r, (2.0 * c) * invk)

    over_rows(*wide, coefficients)
    h_wait(0, 1)
    fine_smooth(gue, u1, steps - 1, steps)
    x_send(1)
    h_wait(3, 4)
    fine_smooth(gue, u1, 1, steps - 1)
    over_planes(1, half, restrict)
    over_planes(half - 1, half, coarse_first)
    x_send(2)
    over_planes(1, half - 1, coarse_first)
    coarse_sweep(e0, e1, half - 1, 0)
    x_send(3)
    over_planes(2, half - 1, lambda m: coarse_sweep(e0, e1, m, 1))
    coarse_sweep(e1, e2, half - 1, 2)
    x_send(4)

    x_wait(0)
    h_send(5)
    h_wait(5)
    fine_smooth(gue, u1, 0, 1)

    x_wait(1)
    h_send(6)
    h_wait(6)
    restrict(0)
    coarse_first(0)
    coarse_sweep(e0, e1, 1, 3)
    coarse_sweep(e1, e2, 2, 4)
    h_send(10)
    h_wait(10)
    prolong_odd(half - 1)
    prolong_even(half - 1)
    fine_smooth(u2, u3, steps - 1, steps)
    x_send(5)
    prolong_odd(half - 2)
    fine_smooth(u2, u3, steps - 2, steps - 1)
    last_residual(steps - 1)

    x_wait(2)
    h_send(7)
    h_wait(7)
    coarse_sweep(e0, e1, 0, 5)
    coarse_sweep(e1, e2, 1, 6)
    h_send(11)
    h_wait(11)
    prolong_even(half - 2)
    prolong_odd(half - 3)
    fine_smooth(u2, u3, steps - 4, steps - 2)
    over_planes(steps - 3, steps - 1, last_residual)

    x_wait(3)
    h_send(8)
    h_wait(8)
    coarse_sweep(e1, e2, 0, 7)
    h_send(12)
    h_wait(12)
    prolong_even(1)
    prolong_odd(0)
    fine_smooth(u2, u3, 2, steps - 4)
    over_planes(3, steps - 3, last_residual)

    x_wait(4)
    h_send(9)
    h_wait(9)
    over_rows(*wide, lambda r: put(u2, 0, r, at(u1, 0, r) + at(e2, 0, r)))
    prolong_even(0)
    fine_smooth(u2, u3, 0, 2)
    over_planes(1, 3, last_residual)

    x_wait(5)
    last_residual(0)

    @pl.when(~last)
    def _():
        for i in range(len(x_plan)):
            x_copy(i, *x_plan[i]).wait_send()

    @pl.when(~bottom)
    def _():
        for i in range(len(h_plan)):
            down_copy(i).wait_send()

    @pl.when(~top)
    def _():
        for i in range(len(h_plan)):
            up_copy(i).wait_send()


def store_kernel(steps, rows, blocks, u3, res, field_out, res_out, sem):
    copies = []
    for k in range(blocks):
        cols = pl.ds(k * LANES, LANES)
        copies.append(
            pltpu.make_async_copy(
                u3.at[pl.ds(1, steps), k, pl.ds(TOP, rows), :], field_out.at[:, :, cols], sem.at[0, k]
            )
        )
        copies.append(pltpu.make_async_copy(res.at[:, k, :, :], res_out.at[:, :, cols], sem.at[1, k]))
    for c in copies:
        c.start()
    for c in copies:
        c.wait()


def shards(source, guess, start_state, conduct):
    steps, rows, cols = source.shape
    blocks = cols // LANES
    half = steps // 2
    tall = rows + 2 * TOP
    f32 = jnp.float32
    hbm = pl.BlockSpec(memory_space=pltpu.HBM)
    vmem = pl.BlockSpec(memory_space=pltpu.VMEM)

    def planes(n):
        return pltpu.VMEM((n, blocks, tall, LANES), f32)

    u3, res = pl.pallas_call(
        functools.partial(cycle_kernel, steps, rows, blocks),
        out_shape=(
            jax.ShapeDtypeStruct((steps + 1, blocks, tall, LANES), f32),
            jax.ShapeDtypeStruct((steps, blocks, rows, LANES), f32),
        ),
        in_specs=[hbm] * 4,
        out_specs=(vmem, vmem),
        scratch_shapes=[
            planes(steps),
            planes(steps + 1),
            planes(steps + 1),
            planes(steps + 1),
            planes(half + 1),
            planes(half + 1),
            planes(half + 1),
            planes(half),
            planes(steps),
            planes(5),
            pltpu.SemaphoreType.DMA((8, blocks)),
            pltpu.SemaphoreType.DMA((6,)),
            pltpu.SemaphoreType.DMA((6,)),
            pltpu.SemaphoreType.DMA((13, 2)),
            pltpu.SemaphoreType.DMA((13, 2)),
        ],
        compiler_params=pltpu.CompilerParams(
            collective_id=0, has_side_effects=True, vmem_limit_bytes=44 * 1024 * 1024
        ),
        name="cycle",
    )(*(pltpu.with_memory_space_constraint(a, pltpu.HBM) for a in (source, guess, start_state, conduct)))
    return pl.pallas_call(
        functools.partial(store_kernel, steps, rows, blocks),
        out_shape=(jax.ShapeDtypeStruct(source.shape, f32), jax.ShapeDtypeStruct(source.shape, f32)),
        in_specs=[vmem, vmem],
        out_specs=(hbm, hbm),
        scratch_shapes=[pltpu.SemaphoreType.DMA((2, blocks))],
        compiler_params=pltpu.CompilerParams(vmem_limit_bytes=16 * 1024 * 1024),
        name="store",
    )(u3, res)


def solution(mesh):
    return jax.shard_map(
        shards,
        mesh=mesh,
        in_specs=(
            P("tm", "space", None),
            P("tm", "space", None),
            P("space", None),
            P("space", None),
        ),
        out_specs=(P("tm", "space", None), P("tm", "space", None)),
        check_vma=False,
    )
```

time: 163 us -> 58.6 us (0.36)
  starting transfers between devices: 80.9 us -> 0 us
  Pallas kernels: 0 us -> 57.7 us
  waiting for transfers between devices: 38.9 us -> 0 us
  other arithmetic: 32.4 us -> 0 us
  local copies, waits for them, and re-layouts: 8.51 us -> 0 us
    ppermute x22 -> x0, starting transfers between devices: 80.9 us -> none  [the longest x8 46.8 us: extended(): lax.ppermute(head, axis, [((i + 1) % count, i) for i in range(ends)])]
    pallas_call x0 -> x2, Pallas kernels: none -> 57.7 us  [the longest x1 55.6 us: shards(): pl.pallas_call(functools.partial(cycle_kernel, steps, rows, blocks), out_...]
    ppermute x22 -> x0, waiting for transfers between devices: 38.9 us -> none  [the longest x6 27.3 us: passed_along(): return lax.ppermute(block, axis, route)]
    div x5 -> x0, other arithmetic: 7.76 us -> none  [the longest x4 7.53 us: widened_smooth(): first_sweep = resid_wide / diagonal]
    add x6 -> x0, other arithmetic: 7.03 us -> none  [the longest x1 2.17 us: shards(): smooth2 + damping * widened_smooth(smooth2, earlier2, source, cond_wide,...]
    concatenate x7 -> x0, other arithmetic: 6.93 us -> none  [extended(): jnp.concatenate([lax.ppermute(tail, axis, [(i, (i + 1) % count) for i in...]
    sub x2 -> x0, other arithmetic: 4.54 us -> none  [fine_residual(): return source + earlier - apply_operator(field, conduct)]
    squeeze x10 -> x0, local copies, waits for them, and re-layouts: 4.39 us -> none  [the longest x4 3.33 us: widened_smooth(): widened[2][:, 1:-1] + widened[1][:, 1:-1]]
  transfers between devices with their start and end apart: 22 -> 0, of which waited for: 15 -> 0; matrix products, arithmetic and copies ran while one was open for 3% -> 0% of each run, Pallas kernels for 0% -> 0%
where the time goes in v1:
time: 58.6 us; the launch traced here: 58.4 us
  Pallas kernels  57.7 us (98%)
  between operations  0.64 us (1%)
    pallas_call x1, Pallas kernels, shards(): pl.pallas_call(functools.partial(cycle_kernel, steps, rows, blocks), out_...  55.6 us
    pallas_call x1, Pallas kernels, shards(): pl.pallas_call(functools.partial(store_kernel, steps, rows, blocks), out_...  2.14 us

profile of v1, /device:TPU:100, one launch (start us, length us, event | category | flops | bytes accessed | tf_op | source)
XLA Modules:
  0.0 58.4 jit_solution(11603781323462685105)
XLA Ops:
  0.6 55.6 %cycle.1 = (f32[9,8,96,128]{3,2,1,0:T(8,128)S(1)}, f32[8,8,64,128]{3,2,1,0:T(8,128)S(1)}) custom-call(f32[8,64,1024]{2,1,0:T(8,128)} %source_hbm.1, f32[8,64,1024]{2,1,0:T(8,128)} %guess_hbm.1, f32[64,1024]{1,0:T(8,128)} %start_hbm.1, f32[64,1024]{1,0:T(8,128)} %cond_hbm.1), custom_call_target="tpu_custom_call" | custom-call | tf_op jit(solution)/shard_map/cycle/pallas_call | solution.py:470
  56.2 2.1 %store.1 = (f32[8,64,1024]{2,1,0:T(8,128)}, f32[8,64,1024]{2,1,0:T(8,128)}) custom-call(f32[9,8,96,128]{3,2,1,0:T(8,128)S(1)} %get-tuple-element.4.u3, f32[8,8,64,128]{3,2,1,0:T(8,128)S(1)} %get-tuple-element.5.res), custom_call_target="tpu_custom_call" | custom-call | tf_op jit(solution)/shard_map/store/pallas_call | solution.py:500

commit v2 on v1

--- a/solution.py
+++ b/solution.py
@@ -58,14 +58,24 @@
             out.append(pltpu.make_async_copy(view, dst, load_sem.at[group, k]))
         return out
 
-    loads = {
-        "g_last": load(0, guess_hbm, steps - 2, gue, steps - 1, 2),
-        "cond": load(1, cond_hbm, None, coef, COND, 1),
-        "s_last": load(2, source_hbm, steps - 2, src, steps - 2, 2),
-        "g_rest": load(3, guess_hbm, 0, gue, 1, steps - 2),
-        "s_rest": load(4, source_hbm, 0, src, 0, steps - 2),
-    }
-    starts = [load(5 + i, start_hbm, None, buf, 0, 1) for i, buf in enumerate((gue, u1, u3))]
+    def guess_load(group, low, count):
+        return load(group, guess_hbm, low, gue, low + 1, count)
+
+    def source_load(group, low, count):
+        return load(group, source_hbm, low, src, low, count)
+
+    loads = [
+        guess_load(0, steps - 2, 2),
+        load(1, cond_hbm, None, coef, COND, 1),
+        source_load(2, steps - 1, 1),
+        guess_load(3, steps - 4, 2),
+        source_load(4, steps - 3, 2),
+        guess_load(5, steps - 6, 2),
+        source_load(6, steps - 5, 2),
+        guess_load(7, 0, 2),
+        source_load(8, 0, 3),
+    ]
+    starts = [load(9 + i, start_hbm, None, buf, 0, 1) for i, buf in enumerate((gue, u1, u3))]
 
     def start(copies):
         for c in copies:
@@ -75,8 +85,8 @@
         for c in copies:
             c.wait()
 
-    for name in ("g_last", "cond", "s_last", "g_rest", "s_rest"):
-        start(loads[name])
+    for copies in loads:
+        start(copies)
 
     @pl.when(first)
     def _():
@@ -136,19 +146,24 @@
 
     h_plan = [
         (gue, steps - 1, 2),
-        (src, steps - 2, 2),
         (coef, COND, 1),
-        (gue, 1, steps - 2),
-        (src, 0, steps - 2),
+        (src, steps - 1, 1),
+        (gue, steps - 3, 2),
+        (src, steps - 3, 2),
+        (gue, steps - 5, 2),
+        (src, steps - 5, 2),
+        (gue, 1, 2),
+        (src, 0, 3),
         (gue, 0, 1),
         (u1, 0, 1),
         (e0, 0, 1),
         (e1, 0, 1),
         (e2, 0, 1),
         (e2, half - 1, 2),
-        (e2, 2, half - 3),
+        (e2, half - 2, 1),
         (e2, 1, 1),
     ]
+    OLD_GUESS, OLD_U1, OLD_E0, OLD_E1, OLD_E2, E2_LATE, E2_MID, E2_EARLY = range(9, 17)
 
     def down_copy(i):
         buf, plane, count = h_plan[i]
@@ -330,17 +345,21 @@
         for buf in (e0, e1, e2):
             buf[0, :, pl.ds(TOP, rows), :] = jnp.zeros((blocks, rows, LANES), jnp.float32)
 
-    wait(loads["g_last"])
+    wait(loads[0])
     x_send(0)
     h_send(0)
-    wait(loads["cond"])
-    wait(loads["s_last"])
-    h_send(2, 1)
-    wait(loads["g_rest"])
-    wait(loads["s_rest"])
+    wait(loads[1])
+    wait(loads[2])
+    h_send(1, 2)
+    wait(loads[3])
+    wait(loads[4])
     h_send(3, 4)
-
-    h_wait(2)
+    wait(loads[5])
+    wait(loads[6])
+    h_send(5, 6)
+    wait(loads[7])
+    wait(loads[8])
+    h_send(7, 8)
 
     def coefficients(r):
         c = at(coef, COND, r)
@@ -351,75 +370,77 @@
         put(coef, INVK, r, invk)
         put(coef, WK, r, (2.0 * c) * invk)
 
+    h_wait(0, 1, 2)
     over_rows(*wide, coefficients)
-    h_wait(0, 1)
     fine_smooth(gue, u1, steps - 1, steps)
     x_send(1)
     h_wait(3, 4)
-    fine_smooth(gue, u1, 1, steps - 1)
-    over_planes(1, half, restrict)
-    over_planes(half - 1, half, coarse_first)
+    fine_smooth(gue, u1, steps - 3, steps - 1)
+    restrict(half - 1)
+    coarse_first(half - 1)
     x_send(2)
-    over_planes(1, half - 1, coarse_first)
+    h_wait(5, 6)
+    fine_smooth(gue, u1, steps - 5, steps - 3)
+    restrict(half - 2)
+    coarse_first(half - 2)
     coarse_sweep(e0, e1, half - 1, 0)
     x_send(3)
-    over_planes(2, half - 1, lambda m: coarse_sweep(e0, e1, m, 1))
+    x_wait(0)
+    h_send(OLD_GUESS)
+    h_wait(7, 8)
+    fine_smooth(gue, u1, 1, steps - 5)
+    restrict(half - 3)
+    coarse_first(half - 3)
+    coarse_sweep(e0, e1, half - 2, 1)
     coarse_sweep(e1, e2, half - 1, 2)
     x_send(4)
-
-    x_wait(0)
-    h_send(5)
-    h_wait(5)
+    h_wait(OLD_GUESS)
     fine_smooth(gue, u1, 0, 1)
 
     x_wait(1)
-    h_send(6)
-    h_wait(6)
+    h_send(OLD_U1)
+    h_wait(OLD_U1)
     restrict(0)
     coarse_first(0)
     coarse_sweep(e0, e1, 1, 3)
     coarse_sweep(e1, e2, 2, 4)
-    h_send(10)
-    h_wait(10)
+    h_send(E2_LATE)
+    x_wait(2)
+    h_send(OLD_E0)
+    h_wait(E2_LATE)
     prolong_odd(half - 1)
     prolong_even(half - 1)
     fine_smooth(u2, u3, steps - 1, steps)
     x_send(5)
+    h_wait(OLD_E0)
+    coarse_sweep(e0, e1, 0, 5)
+    coarse_sweep(e1, e2, 1, 6)
+    h_send(E2_MID)
     prolong_odd(half - 2)
     fine_smooth(u2, u3, steps - 2, steps - 1)
     last_residual(steps - 1)
-
-    x_wait(2)
-    h_send(7)
-    h_wait(7)
-    coarse_sweep(e0, e1, 0, 5)
-    coarse_sweep(e1, e2, 1, 6)
-    h_send(11)
-    h_wait(11)
+    x_wait(3)
+    h_send(OLD_E1)
+    h_wait(E2_MID)
     prolong_even(half - 2)
     prolong_odd(half - 3)
     fine_smooth(u2, u3, steps - 4, steps - 2)
+    h_wait(OLD_E1)
+    coarse_sweep(e1, e2, 0, 7)
+    h_send(E2_EARLY)
     over_planes(steps - 3, steps - 1, last_residual)
-
-    x_wait(3)
-    h_send(8)
-    h_wait(8)
-    coarse_sweep(e1, e2, 0, 7)
-    h_send(12)
-    h_wait(12)
+    x_wait(4)
+    h_send(OLD_E2)
+    h_wait(E2_EARLY)
     prolong_even(1)
     prolong_odd(0)
     fine_smooth(u2, u3, 2, steps - 4)
     over_planes(3, steps - 3, last_residual)
-
-    x_wait(4)
-    h_send(9)
-    h_wait(9)
+    h_wait(OLD_E2)
     over_rows(*wide, lambda r: put(u2, 0, r, at(u1, 0, r) + at(e2, 0, r)))
     prolong_even(0)
     fine_smooth(u2, u3, 0, 2)
     over_planes(1, 3, last_residual)
-
     x_wait(5)
     last_residual(0)
 
@@ -486,11 +507,11 @@
             planes(half),
             planes(steps),
             planes(5),
-            pltpu.SemaphoreType.DMA((8, blocks)),
+            pltpu.SemaphoreType.DMA((12, blocks)),
             pltpu.SemaphoreType.DMA((6,)),
             pltpu.SemaphoreType.DMA((6,)),
-            pltpu.SemaphoreType.DMA((13, 2)),
-            pltpu.SemaphoreType.DMA((13, 2)),
+            pltpu.SemaphoreType.DMA((17, 2)),
+            pltpu.SemaphoreType.DMA((17, 2)),
         ],
         compiler_params=pltpu.CompilerParams(
             collective_id=0, has_side_effects=True, vmem_limit_bytes=44 * 1024 * 1024

time: 58.6 us -> 42.5 us (0.73)
  Pallas kernels: 57.7 us -> 41.4 us
    pallas_call x1, Pallas kernels: 55.6 us -> 39.2 us  [shards(): pl.pallas_call(functools.partial(cycle_kernel, steps, rows, blocks), out_...]
where the time goes in v2:
time: 42.5 us; the launch traced here: 42 us
  Pallas kernels  41.4 us (97%)
  between operations  0.64 us (2%)
    pallas_call x1, Pallas kernels, shards(): pl.pallas_call(functools.partial(cycle_kernel, steps, rows, blocks), out_...  39.2 us
    pallas_call x1, Pallas kernels, shards(): pl.pallas_call(functools.partial(store_kernel, steps, rows, blocks), out_...  2.14 us

profile of v2, /device:TPU:100, one launch (start us, length us, event | category | flops | bytes accessed | tf_op | source)
XLA Modules:
  0.0 42.0 jit_solution(6260393920247076402)
XLA Ops:
  0.6 39.2 %cycle.1 = (f32[9,8,96,128]{3,2,1,0:T(8,128)S(1)}, f32[8,8,64,128]{3,2,1,0:T(8,128)S(1)}) custom-call(f32[8,64,1024]{2,1,0:T(8,128)} %source_hbm.1, f32[8,64,1024]{2,1,0:T(8,128)} %guess_hbm.1, f32[64,1024]{1,0:T(8,128)} %start_hbm.1, f32[64,1024]{1,0:T(8,128)} %cond_hbm.1), custom_call_target="tpu_custom_call" | custom-call | tf_op jit(solution)/shard_map/cycle/pallas_call | solution.py:491
  39.9 2.1 %store.1 = (f32[8,64,1024]{2,1,0:T(8,128)}, f32[8,64,1024]{2,1,0:T(8,128)}) custom-call(f32[9,8,96,128]{3,2,1,0:T(8,128)S(1)} %get-tuple-element.4.u3, f32[8,8,64,128]{3,2,1,0:T(8,128)S(1)} %get-tuple-element.5.res), custom_call_target="tpu_custom_call" | custom-call | tf_op jit(solution)/shard_map/store/pallas_call | solution.py:521

commit v3 on v2

--- a/solution.py
+++ b/solution.py
@@ -10,9 +10,10 @@
 damping = 0.8
 MESH = pl.DeviceIdType.MESH
 LANES = 128
-HALO = 8
+HALO = 12
 TOP = 16
-CHUNK = 16
+CHUNK = 8
+EDGE = 24
 
 
 def cycle_kernel(
@@ -35,9 +36,14 @@
     rhs,
     tmp,
     coef,
+    sums,
+    relay,
     load_sem,
     xs,
     xr,
+    ls,
+    lr,
+    fs,
     hs,
     hr,
 ):
@@ -75,7 +81,7 @@
         guess_load(7, 0, 2),
         source_load(8, 0, 3),
     ]
-    starts = [load(9 + i, start_hbm, None, buf, 0, 1) for i, buf in enumerate((gue, u1, u3))]
+    starts = [load(9 + i, start_hbm, None, buf, 0, 1) for i, buf in enumerate((gue, u3))]
 
     def start(copies):
         for c in copies:
@@ -100,76 +106,119 @@
         def _():
             pl.semaphore_signal(barrier, inc=1, device_id={axis: index}, device_id_type=MESH)
 
-    greet(~first, "tm", tm - 1)
-    greet(~last, "tm", tm + 1)
+    for other in range(n_tm):
+        greet(tm != other, "tm", other)
     greet(~top, "space", sp - 1)
     greet(~bottom, "space", sp + 1)
     one = jnp.int32(1)
     zero = jnp.int32(0)
-    peers = (
-        jnp.where(first, zero, one)
-        + jnp.where(last, zero, one)
-        + jnp.where(top, zero, one)
-        + jnp.where(bottom, zero, one)
-    )
-    pl.semaphore_wait(barrier, peers)
-
-    own = pl.ds(TOP, rows)
-
-    def x_copy(i, buf, plane):
+    pl.semaphore_wait(barrier, (n_tm - 1) + jnp.where(top, zero, one) + jnp.where(bottom, zero, one))
+
+    x_plan = [(gue, steps), (sums, 1), (e0, half), (e1, half), (e2, half), (u3, steps)]
+    pieces = [(TOP, EDGE), (end - EDGE, EDGE), (TOP + EDGE, rows - 2 * EDGE)]
+    MIDDLE = 2
+    relayed = {1: 0, 2: 1, 3: 2, 5: 3}
+    ways = {0: (3, 0), 1: (3, 1), 2: (1, 0)}
+    relays = {3: ((0, 1), (1, 2)), 1: ((0, 3),)}
+
+    def x_copy(i, piece):
+        buf, plane = x_plan[i]
+        part = pl.ds(*pieces[piece])
         return pltpu.make_async_remote_copy(
-            src_ref=buf.at[plane, :, own, :],
-            dst_ref=buf.at[0, :, own, :],
-            send_sem=xs.at[i],
-            recv_sem=xr.at[i],
+            src_ref=buf.at[plane, :, part, :],
+            dst_ref=buf.at[0, :, part, :],
+            send_sem=xs.at[i, piece],
+            recv_sem=xr.at[i, piece],
             device_id={"tm": tm + 1},
             device_id_type=MESH,
         )
 
-    x_plan = [(gue, steps), (u1, steps), (e0, half), (e1, half), (e2, half), (u3, steps)]
+    def to_relay(i, device, slot):
+        buf, plane = x_plan[i]
+        return pltpu.make_async_remote_copy(
+            src_ref=buf.at[plane, :, pl.ds(*pieces[MIDDLE]), :],
+            dst_ref=relay.at[slot, relayed[i]],
+            send_sem=ls.at[relayed[i]],
+            recv_sem=lr.at[slot, relayed[i]],
+            device_id={"tm": device},
+            device_id_type=MESH,
+        )
+
+    def from_relay(i, slot, device):
+        return pltpu.make_async_remote_copy(
+            src_ref=relay.at[slot, relayed[i]],
+            dst_ref=x_plan[i][0].at[0, :, pl.ds(*pieces[MIDDLE]), :],
+            send_sem=fs.at[slot, relayed[i]],
+            recv_sem=xr.at[i, MIDDLE],
+            device_id={"tm": device},
+            device_id_type=MESH,
+        )
+
+    def direct(i):
+        return (0, 1) if i in relayed else (0, 1, 2)
 
     def x_send(i):
+        if i in relayed:
+            for sender, way in ways.items():
+
+                @pl.when(tm == sender)
+                def _():
+                    to_relay(i, *way).start()
+
         @pl.when(~last)
         def _():
-            x_copy(i, *x_plan[i]).start()
-
-    def x_wait(i):
+            for piece in direct(i):
+                x_copy(i, piece).start()
+
+    def x_relay(i):
+        for device, jobs in relays.items():
+
+            @pl.when(tm == device)
+            def _():
+                for slot, final in jobs:
+                    to_relay(i, device, slot).wait_recv()
+                    from_relay(i, slot, final).start()
+
+    def x_edges(i):
         @pl.when(~first)
         def _():
-            x_copy(i, *x_plan[i]).wait_recv()
-
-        if i in (0, 1, 5):
+            for piece in (0, 1):
+                x_copy(i, piece).wait_recv()
+
+        if i in (0, 5):
 
             @pl.when(first)
             def _():
-                wait(starts[(0, 1, 5).index(i)])
+                wait(starts[(0, 5).index(i)])
+
+    def x_middle(i):
+        @pl.when(~first)
+        def _():
+            x_copy(i, MIDDLE).wait_recv()
 
     h_plan = [
-        (gue, steps - 1, 2),
-        (coef, COND, 1),
-        (src, steps - 1, 1),
-        (gue, steps - 3, 2),
-        (src, steps - 3, 2),
-        (gue, steps - 5, 2),
-        (src, steps - 5, 2),
-        (gue, 1, 2),
-        (src, 0, 3),
-        (gue, 0, 1),
-        (u1, 0, 1),
-        (e0, 0, 1),
-        (e1, 0, 1),
-        (e2, 0, 1),
-        (e2, half - 1, 2),
-        (e2, half - 2, 1),
-        (e2, 1, 1),
+        (gue, steps - 1, 2, 11),
+        (coef, COND, 1, 10),
+        (src, steps - 1, 1, 10),
+        (gue, steps - 3, 2, 11),
+        (src, steps - 3, 2, 10),
+        (gue, steps - 5, 2, 11),
+        (src, steps - 5, 2, 10),
+        (gue, 1, 2, 11),
+        (src, 0, 3, 10),
+        (gue, 0, 1, 10),
+        (sums, 0, 1, 9),
+        (e0, 0, 1, 6),
+        (e1, 0, 1, 4),
+        (e2, 0, 1, 3),
     ]
-    OLD_GUESS, OLD_U1, OLD_E0, OLD_E1, OLD_E2, E2_LATE, E2_MID, E2_EARLY = range(9, 17)
+    OLD_GUESS, OLD_SUM, OLD_E0, OLD_E1, OLD_E2 = range(9, 14)
 
     def down_copy(i):
-        buf, plane, count = h_plan[i]
+        buf, plane, count, width = h_plan[i]
         return pltpu.make_async_remote_copy(
-            src_ref=buf.at[pl.ds(plane, count), :, pl.ds(end - HALO, HALO), :],
-            dst_ref=buf.at[pl.ds(plane, count), :, pl.ds(TOP - HALO, HALO), :],
+            src_ref=buf.at[pl.ds(plane, count), :, pl.ds(end - width, width), :],
+            dst_ref=buf.at[pl.ds(plane, count), :, pl.ds(TOP - width, width), :],
             send_sem=hs.at[i, 0],
             recv_sem=hr.at[i, 0],
             device_id={"space": sp + 1},
@@ -177,10 +226,10 @@
         )
 
     def up_copy(i):
-        buf, plane, count = h_plan[i]
+        buf, plane, count, width = h_plan[i]
         return pltpu.make_async_remote_copy(
-            src_ref=buf.at[pl.ds(plane, count), :, pl.ds(TOP, HALO), :],
-            dst_ref=buf.at[pl.ds(plane, count), :, pl.ds(end, HALO), :],
+            src_ref=buf.at[pl.ds(plane, count), :, pl.ds(TOP, width), :],
+            dst_ref=buf.at[pl.ds(plane, count), :, pl.ds(end, width), :],
             send_sem=hs.at[i, 1],
             recv_sem=hr.at[i, 1],
             device_id={"space": sp - 1},
@@ -248,26 +297,47 @@
 
             lax.fori_loop(low, high, step, 0)
 
-    wide = (TOP - HALO, end + HALO)
-
-    def fine_smooth(frm, to, low, high):
+    def grown(extra):
+        return (TOP - extra, end + extra)
+
+    fine_rows, coarse_rows, late_rows = grown(12), grown(8), grown(4)
+
+    def fine_smooth(frm, to, low, high, where):
         def first_pass(n):
             def chunk(r):
                 v, s = with_sum(frm, n + 1, r)
                 rest = at(src, n, r) + at(frm, n, r)
                 put(tmp, n, r, damping * (at(coef, INV, r) * rest + at(coef, W, r) * s - v))
 
-            over_rows(*wide, chunk)
+            over_rows(*where, chunk)
 
         def second_pass(n):
             def chunk(r):
                 v, s = with_sum(tmp, n, r)
                 put(to, n + 1, r, at(frm, n + 1, r) + (v + at(coef, W, r) * s))
 
-            over_rows(*wide, chunk)
+            over_rows(*where, chunk)
 
         over_planes(low, high, first_pass)
         over_planes(low, high, second_pass)
+
+    def smooth_before():
+        def first_pass(r):
+            v, s = with_sum(gue, 0, r)
+            put(tmp, 0, r, damping * (at(coef, INV, r) * at(sums, 0, r) + at(coef, W, r) * s - v))
+
+        def second_pass(r):
+            v, s = with_sum(tmp, 0, r)
+            put(u1, 0, r, at(gue, 0, r) + (v + at(coef, W, r) * s))
+
+        @pl.when(first)
+        def _():
+            over_rows(*fine_rows, lambda r: put(u1, 0, r, at(gue, 0, r)))
+
+        @pl.when(~first)
+        def _():
+            over_rows(*fine_rows, first_pass)
+            over_rows(*fine_rows, second_pass)
 
     def restrict(m):
         def chunk(r):
@@ -279,14 +349,14 @@
             total = total - at(coef, COND, r) * (4.0 * pair - around)
             put(rhs, m, r, at(coef, INVK, r) * total)
 
-        over_rows(*wide, chunk)
+        over_rows(*coarse_rows, chunk)
 
     def coarse_first(m):
         def chunk(r):
             v, s = with_sum(rhs, m, r)
             put(e0, m + 1, r, damping * (v + at(coef, WK, r) * s))
 
-        over_rows(*wide, chunk)
+        over_rows(*coarse_rows, chunk)
 
     def coarse_sweep(frm, to, m, slot):
         def first_pass(r):
@@ -298,15 +368,16 @@
             v, s = with_sum(tmp, slot, r)
             put(to, m + 1, r, at(frm, m + 1, r) + (v + at(coef, WK, r) * s))
 
-        over_rows(*wide, first_pass)
-        over_rows(*((TOP, end) if to is e2 else wide), second_pass)
+        where = late_rows if to is e2 else coarse_rows
+        over_rows(*where, first_pass)
+        over_rows(*where, second_pass)
 
     def prolong_odd(m):
-        over_rows(*wide, lambda r: put(u2, 2 * m + 2, r, at(u1, 2 * m + 2, r) + at(e2, m + 1, r)))
+        over_rows(*late_rows, lambda r: put(u2, 2 * m + 2, r, at(u1, 2 * m + 2, r) + at(e2, m + 1, r)))
 
     def prolong_even(m):
         over_rows(
-            *wide,
+            *late_rows,
             lambda r: put(u2, 2 * m + 1, r, at(u1, 2 * m + 1, r) + 0.5 * (at(e2, m, r) + at(e2, m + 1, r))),
         )
 
@@ -328,9 +399,8 @@
         planes(gue, 0, steps + 1)
         planes(src, 0, steps)
         planes(coef, COND, COND + 1)
-        for buf in (u1, e0, e1):
+        for buf in (sums, e0, e1, e2):
             planes(buf, 0, 1)
-        planes(e2, 0, half + 1)
 
     @pl.when(top)
     def _():
@@ -342,7 +412,7 @@
 
     @pl.when(first)
     def _():
-        for buf in (e0, e1, e2):
+        for buf in (sums, e0, e1, e2):
             buf[0, :, pl.ds(TOP, rows), :] = jnp.zeros((blocks, rows, LANES), jnp.float32)
 
     wait(loads[0])
@@ -350,7 +420,9 @@
     h_send(0)
     wait(loads[1])
     wait(loads[2])
+    over_rows(TOP, end, lambda r: put(sums, 1, r, at(src, steps - 1, r) + at(gue, steps - 1, r)))
     h_send(1, 2)
+    x_send(1)
     wait(loads[3])
     wait(loads[4])
     h_send(3, 4)
@@ -371,83 +443,98 @@
         put(coef, WK, r, (2.0 * c) * invk)
 
     h_wait(0, 1, 2)
-    over_rows(*wide, coefficients)
-    fine_smooth(gue, u1, steps - 1, steps)
-    x_send(1)
+    over_rows(*fine_rows, coefficients)
+    fine_smooth(gue, u1, steps - 1, steps, fine_rows)
     h_wait(3, 4)
-    fine_smooth(gue, u1, steps - 3, steps - 1)
+    fine_smooth(gue, u1, steps - 3, steps - 1, fine_rows)
     restrict(half - 1)
     coarse_first(half - 1)
     x_send(2)
+    x_edges(0)
+    h_send(OLD_GUESS)
+    x_relay(1)
     h_wait(5, 6)
-    fine_smooth(gue, u1, steps - 5, steps - 3)
+    fine_smooth(gue, u1, steps - 5, steps - 3, fine_rows)
     restrict(half - 2)
     coarse_first(half - 2)
     coarse_sweep(e0, e1, half - 1, 0)
     x_send(3)
-    x_wait(0)
-    h_send(OLD_GUESS)
+    x_edges(1)
+    h_send(OLD_SUM)
     h_wait(7, 8)
-    fine_smooth(gue, u1, 1, steps - 5)
+    fine_smooth(gue, u1, 1, steps - 5, fine_rows)
     restrict(half - 3)
     coarse_first(half - 3)
     coarse_sweep(e0, e1, half - 2, 1)
     coarse_sweep(e1, e2, half - 1, 2)
     x_send(4)
     h_wait(OLD_GUESS)
-    fine_smooth(gue, u1, 0, 1)
-
-    x_wait(1)
-    h_send(OLD_U1)
-    h_wait(OLD_U1)
+    x_middle(0)
+    fine_smooth(gue, u1, 0, 1, fine_rows)
+
+    h_wait(OLD_SUM)
+    x_middle(1)
+    smooth_before()
     restrict(0)
     coarse_first(0)
+    x_edges(2)
+    h_send(OLD_E0)
     coarse_sweep(e0, e1, 1, 3)
     coarse_sweep(e1, e2, 2, 4)
-    h_send(E2_LATE)
-    x_wait(2)
-    h_send(OLD_E0)
-    h_wait(E2_LATE)
+    x_relay(2)
     prolong_odd(half - 1)
     prolong_even(half - 1)
-    fine_smooth(u2, u3, steps - 1, steps)
+    fine_smooth(u2, u3, steps - 1, steps, late_rows)
     x_send(5)
+    prolong_odd(half - 2)
+    fine_smooth(u2, u3, steps - 2, steps - 1, late_rows)
+    last_residual(steps - 1)
+    x_relay(3)
+    x_edges(3)
+    h_send(OLD_E1)
     h_wait(OLD_E0)
+    x_middle(2)
     coarse_sweep(e0, e1, 0, 5)
     coarse_sweep(e1, e2, 1, 6)
-    h_send(E2_MID)
-    prolong_odd(half - 2)
-    fine_smooth(u2, u3, steps - 2, steps - 1)
-    last_residual(steps - 1)
-    x_wait(3)
-    h_send(OLD_E1)
-    h_wait(E2_MID)
     prolong_even(half - 2)
     prolong_odd(half - 3)
-    fine_smooth(u2, u3, steps - 4, steps - 2)
+    fine_smooth(u2, u3, steps - 4, steps - 2, late_rows)
     h_wait(OLD_E1)
+    x_middle(3)
     coarse_sweep(e1, e2, 0, 7)
-    h_send(E2_EARLY)
+    x_edges(4)
+    h_send(OLD_E2)
+    x_relay(5)
     over_planes(steps - 3, steps - 1, last_residual)
-    x_wait(4)
-    h_send(OLD_E2)
-    h_wait(E2_EARLY)
     prolong_even(1)
     prolong_odd(0)
-    fine_smooth(u2, u3, 2, steps - 4)
+    fine_smooth(u2, u3, 2, steps - 4, late_rows)
     over_planes(3, steps - 3, last_residual)
     h_wait(OLD_E2)
-    over_rows(*wide, lambda r: put(u2, 0, r, at(u1, 0, r) + at(e2, 0, r)))
+    x_middle(4)
+    over_rows(*late_rows, lambda r: put(u2, 0, r, at(u1, 0, r) + at(e2, 0, r)))
     prolong_even(0)
-    fine_smooth(u2, u3, 0, 2)
+    fine_smooth(u2, u3, 0, 2, late_rows)
     over_planes(1, 3, last_residual)
-    x_wait(5)
+    x_edges(5)
+    x_middle(5)
     last_residual(0)
 
     @pl.when(~last)
     def _():
         for i in range(len(x_plan)):
-            x_copy(i, *x_plan[i]).wait_send()
+            for piece in direct(i):
+                x_copy(i, piece).wait_send()
+        for i in relayed:
+            to_relay(i, 0, 0).wait_send()
+
+    for device, jobs in relays.items():
+
+        @pl.when(tm == device)
+        def _():
+            for i in relayed:
+                for slot, final in jobs:
+                    from_relay(i, slot, final).wait_send()
 
     @pl.when(~bottom)
     def _():
@@ -507,11 +594,16 @@
             planes(half),
             planes(steps),
             planes(5),
-            pltpu.SemaphoreType.DMA((12, blocks)),
-            pltpu.SemaphoreType.DMA((6,)),
-            pltpu.SemaphoreType.DMA((6,)),
-            pltpu.SemaphoreType.DMA((17, 2)),
-            pltpu.SemaphoreType.DMA((17, 2)),
+            planes(2),
+            pltpu.VMEM((2, 4, blocks, rows - 2 * EDGE, LANES), f32),
+            pltpu.SemaphoreType.DMA((11, blocks)),
+            pltpu.SemaphoreType.DMA((6, 3)),
+            pltpu.SemaphoreType.DMA((6, 3)),
+            pltpu.SemaphoreType.DMA((4,)),
+            pltpu.SemaphoreType.DMA((2, 4)),
+            pltpu.SemaphoreType.DMA((2, 4)),
+            pltpu.SemaphoreType.DMA((14, 2)),
+            pltpu.SemaphoreType.DMA((14, 2)),
         ],
         compiler_params=pltpu.CompilerParams(
             collective_id=0, has_side_effects=True, vmem_limit_bytes=44 * 1024 * 1024

time: 42.5 us -> 38.3 us (0.901)
  Pallas kernels: 41.4 us -> 37.4 us
    pallas_call x1, Pallas kernels: 39.2 us -> 35.3 us  [shards(): pl.pallas_call(functools.partial(cycle_kernel, steps, rows, blocks), out_...]
where the time goes in v3:
time: 38.3 us; the launch traced here: 38.2 us
  Pallas kernels  37.4 us (98%)
  between operations  0.8 us (2%)
    pallas_call x1, Pallas kernels, shards(): pl.pallas_call(functools.partial(cycle_kernel, steps, rows, blocks), out_...  35.3 us
    pallas_call x1, Pallas kernels, shards(): pl.pallas_call(functools.partial(store_kernel, steps, rows, blocks), out_...  2.14 us

profile of v3, /device:TPU:100, one launch (start us, length us, event | category | flops | bytes accessed | tf_op | source)
XLA Modules:
  0.0 38.2 jit_solution(90312263911479219)
XLA Ops:
  0.6 35.3 %cycle.1 = (f32[9,8,96,128]{3,2,1,0:T(8,128)S(1)}, f32[8,8,64,128]{3,2,1,0:T(8,128)S(1)}) custom-call(f32[8,64,1024]{2,1,0:T(8,128)} %source_hbm.1, f32[8,64,1024]{2,1,0:T(8,128)} %guess_hbm.1, f32[64,1024]{1,0:T(8,128)} %start_hbm.1, f32[64,1024]{1,0:T(8,128)} %cond_hbm.1), custom_call_target="tpu_custom_call" | custom-call | tf_op jit(solution)/shard_map/cycle/pallas_call | solution.py:578
  35.9 2.1 %store.1 = (f32[8,64,1024]{2,1,0:T(8,128)}, f32[8,64,1024]{2,1,0:T(8,128)}) custom-call(f32[9,8,96,128]{3,2,1,0:T(8,128)S(1)} %get-tuple-element.4.u3, f32[8,8,64,128]{3,2,1,0:T(8,128)S(1)} %get-tuple-element.5.res), custom_call_target="tpu_custom_call" | custom-call | tf_op jit(solution)/shard_map/store/pallas_call | solution.py:613

commit v4 on v3

--- a/solution.py
+++ b/solution.py
@@ -13,7 +13,8 @@
 HALO = 12
 TOP = 16
 CHUNK = 8
-EDGE = 24
+EDGE = (12, 12, 8, 8, 8, 8)
+AROUND = (8, 16, 8, 12, 12, 16)
 
 
 def cycle_kernel(
@@ -41,7 +42,6 @@
     load_sem,
     xs,
     xr,
-    ls,
     lr,
     fs,
     hs,
@@ -55,13 +55,18 @@
     top, bottom = sp == 0, sp == n_sp - 1
     COND, INV, W, INVK, WK = range(5)
 
+    def rows_wait(sem, count):
+        planes = next(n for n in range(1, count + 1) if count % n == 0 and count // n <= end)
+        there = gue.at[pl.ds(0, planes), :, pl.ds(0, count // planes), :]
+        pltpu.make_async_copy(there, there, sem).wait()
+
     def load(group, hbm, lead, buf, at, count):
         out = []
         for k in range(blocks):
             cols = pl.ds(k * LANES, LANES)
             view = hbm.at[:, cols] if lead is None else hbm.at[pl.ds(lead, count), :, cols]
             dst = buf.at[at, k, pl.ds(TOP, rows), :] if lead is None else buf.at[pl.ds(at, count), k, pl.ds(TOP, rows), :]
-            out.append(pltpu.make_async_copy(view, dst, load_sem.at[group, k]))
+            out.append(pltpu.make_async_copy(view, dst, load_sem.at[group]))
         return out
 
     def guess_load(group, low, count):
@@ -70,34 +75,28 @@
     def source_load(group, low, count):
         return load(group, source_hbm, low, src, low, count)
 
-    loads = [
+    def load_wait(group):
+        rows_wait(load_sem.at[group], rows * (2, 2, 4, 4, 5, 1, 1)[group])
+
+    for copies in (
         guess_load(0, steps - 2, 2),
         load(1, cond_hbm, None, coef, COND, 1),
-        source_load(2, steps - 1, 1),
-        guess_load(3, steps - 4, 2),
-        source_load(4, steps - 3, 2),
-        guess_load(5, steps - 6, 2),
-        source_load(6, steps - 5, 2),
-        guess_load(7, 0, 2),
-        source_load(8, 0, 3),
-    ]
-    starts = [load(9 + i, start_hbm, None, buf, 0, 1) for i, buf in enumerate((gue, u3))]
-
-    def start(copies):
+        source_load(1, steps - 1, 1),
+        guess_load(2, steps - 4, 2),
+        source_load(2, steps - 3, 2),
+        guess_load(3, steps - 6, 2),
+        source_load(3, steps - 5, 2),
+        guess_load(4, 0, 2),
+        source_load(4, 0, 3),
+    ):
         for c in copies:
             c.start()
 
-    def wait(copies):
-        for c in copies:
-            c.wait()
-
-    for copies in loads:
-        start(copies)
-
     @pl.when(first)
     def _():
-        for copies in starts:
-            start(copies)
+        for i, buf in enumerate((gue, u3)):
+            for c in load(5 + i, start_hbm, None, buf, 0, 1):
+                c.start()
 
     barrier = pltpu.get_barrier_semaphore()
 
@@ -107,28 +106,32 @@
             pl.semaphore_signal(barrier, inc=1, device_id={axis: index}, device_id_type=MESH)
 
     for other in range(n_tm):
-        greet(tm != other, "tm", other)
+        greet((tm != other) & (tm + other != 2), "tm", other)
     greet(~top, "space", sp - 1)
     greet(~bottom, "space", sp + 1)
     one = jnp.int32(1)
     zero = jnp.int32(0)
-    pl.semaphore_wait(barrier, (n_tm - 1) + jnp.where(top, zero, one) + jnp.where(bottom, zero, one))
+    peers = jnp.where((tm == 1) | (tm == 3), one * 3, one * 2)
+    pl.semaphore_wait(barrier, peers + jnp.where(top, zero, one) + jnp.where(bottom, zero, one))
 
     x_plan = [(gue, steps), (sums, 1), (e0, half), (e1, half), (e2, half), (u3, steps)]
-    pieces = [(TOP, EDGE), (end - EDGE, EDGE), (TOP + EDGE, rows - 2 * EDGE)]
-    MIDDLE = 2
-    relayed = {1: 0, 2: 1, 3: 2, 5: 3}
     ways = {0: (3, 0), 1: (3, 1), 2: (1, 0)}
     relays = {3: ((0, 1), (1, 2)), 1: ((0, 3),)}
+    FIRST_ROWS, LAST_ROWS, INNER, AROUND_ROWS = range(4)
+
+    def part(i, piece):
+        edge, inner = EDGE[i], rows - 2 * EDGE[i] - AROUND[i]
+        return pl.ds(
+            *((TOP, edge), (end - edge, edge), (TOP + edge, inner), (TOP + edge + inner, AROUND[i]))[piece]
+        )
 
     def x_copy(i, piece):
         buf, plane = x_plan[i]
-        part = pl.ds(*pieces[piece])
         return pltpu.make_async_remote_copy(
-            src_ref=buf.at[plane, :, part, :],
-            dst_ref=buf.at[0, :, part, :],
-            send_sem=xs.at[i, piece],
-            recv_sem=xr.at[i, piece],
+            src_ref=buf.at[plane, :, part(i, piece), :],
+            dst_ref=buf.at[0, :, part(i, piece), :],
+            send_sem=xs,
+            recv_sem=xr.at[i, piece // 2],
             device_id={"tm": tm + 1},
             device_id_type=MESH,
         )
@@ -136,39 +139,45 @@
     def to_relay(i, device, slot):
         buf, plane = x_plan[i]
         return pltpu.make_async_remote_copy(
-            src_ref=buf.at[plane, :, pl.ds(*pieces[MIDDLE]), :],
-            dst_ref=relay.at[slot, relayed[i]],
-            send_sem=ls.at[relayed[i]],
-            recv_sem=lr.at[slot, relayed[i]],
+            src_ref=buf.at[plane, :, part(i, AROUND_ROWS), :],
+            dst_ref=relay.at[slot, i, :, pl.ds(0, AROUND[i]), :],
+            send_sem=xs,
+            recv_sem=lr.at[slot, i],
             device_id={"tm": device},
             device_id_type=MESH,
         )
 
     def from_relay(i, slot, device):
         return pltpu.make_async_remote_copy(
-            src_ref=relay.at[slot, relayed[i]],
-            dst_ref=x_plan[i][0].at[0, :, pl.ds(*pieces[MIDDLE]), :],
-            send_sem=fs.at[slot, relayed[i]],
-            recv_sem=xr.at[i, MIDDLE],
+            src_ref=relay.at[slot, i, :, pl.ds(0, AROUND[i]), :],
+            dst_ref=x_plan[i][0].at[0, :, part(i, AROUND_ROWS), :],
+            send_sem=fs.at[slot],
+            recv_sem=xr.at[i, 1],
             device_id={"tm": device},
             device_id_type=MESH,
         )
 
-    def direct(i):
-        return (0, 1) if i in relayed else (0, 1, 2)
+    def x_send_edges(i):
+        @pl.when(~last)
+        def _():
+            x_copy(i, FIRST_ROWS).start()
+            x_copy(i, LAST_ROWS).start()
+
+        for sender, way in ways.items():
+
+            @pl.when(tm == sender)
+            def _():
+                to_relay(i, *way).start()
+
+    def x_send_inner(*which):
+        @pl.when(~last)
+        def _():
+            for i in which:
+                x_copy(i, INNER).start()
 
     def x_send(i):
-        if i in relayed:
-            for sender, way in ways.items():
-
-                @pl.when(tm == sender)
-                def _():
-                    to_relay(i, *way).start()
-
-        @pl.when(~last)
-        def _():
-            for piece in direct(i):
-                x_copy(i, piece).start()
+        x_send_edges(i)
+        x_send_inner(i)
 
     def x_relay(i):
         for device, jobs in relays.items():
@@ -182,81 +191,74 @@
     def x_edges(i):
         @pl.when(~first)
         def _():
-            for piece in (0, 1):
-                x_copy(i, piece).wait_recv()
+            rows_wait(xr.at[i, 0], 2 * EDGE[i])
 
         if i in (0, 5):
 
             @pl.when(first)
             def _():
-                wait(starts[(0, 5).index(i)])
-
-    def x_middle(i):
+                load_wait(5 if i == 0 else 6)
+
+    def x_inner(i):
         @pl.when(~first)
         def _():
-            x_copy(i, MIDDLE).wait_recv()
+            rows_wait(xr.at[i, 1], rows - 2 * EDGE[i])
 
     h_plan = [
-        (gue, steps - 1, 2, 11),
-        (coef, COND, 1, 10),
-        (src, steps - 1, 1, 10),
-        (gue, steps - 3, 2, 11),
-        (src, steps - 3, 2, 10),
-        (gue, steps - 5, 2, 11),
-        (src, steps - 5, 2, 10),
-        (gue, 1, 2, 11),
-        (src, 0, 3, 10),
-        (gue, 0, 1, 10),
-        (sums, 0, 1, 9),
-        (e0, 0, 1, 6),
-        (e1, 0, 1, 4),
-        (e2, 0, 1, 3),
+        ((gue, steps - 1, 2, 11), (coef, COND, 1, 10), (src, steps - 1, 1, 10)),
+        ((gue, steps - 3, 2, 11), (src, steps - 3, 2, 10)),
+        ((gue, steps - 5, 2, 11), (src, steps - 5, 2, 10)),
+        ((gue, 1, 2, 11), (src, 0, 3, 10)),
+        ((gue, 0, 1, 10),),
+        ((sums, 0, 1, 9),),
+        ((e0, 0, 1, 6),),
+        ((e1, 0, 1, 4),),
+        ((e2, 0, 1, 3),),
     ]
-    OLD_GUESS, OLD_SUM, OLD_E0, OLD_E1, OLD_E2 = range(9, 14)
-
-    def down_copy(i):
-        buf, plane, count, width = h_plan[i]
+    OLD_GUESS, OLD_SUM, OLD_E0, OLD_E1, OLD_E2 = range(4, 9)
+
+    def down_copy(i, buf, plane, count, width):
         return pltpu.make_async_remote_copy(
             src_ref=buf.at[pl.ds(plane, count), :, pl.ds(end - width, width), :],
             dst_ref=buf.at[pl.ds(plane, count), :, pl.ds(TOP - width, width), :],
-            send_sem=hs.at[i, 0],
+            send_sem=hs.at[0],
             recv_sem=hr.at[i, 0],
             device_id={"space": sp + 1},
             device_id_type=MESH,
         )
 
-    def up_copy(i):
-        buf, plane, count, width = h_plan[i]
+    def up_copy(i, buf, plane, count, width):
         return pltpu.make_async_remote_copy(
             src_ref=buf.at[pl.ds(plane, count), :, pl.ds(TOP, width), :],
             dst_ref=buf.at[pl.ds(plane, count), :, pl.ds(end, width), :],
-            send_sem=hs.at[i, 1],
+            send_sem=hs.at[1],
             recv_sem=hr.at[i, 1],
             device_id={"space": sp - 1},
             device_id_type=MESH,
         )
 
-    def h_send(*which):
+    def h_send(i, low=0, high=9):
         @pl.when(~bottom)
         def _():
-            for i in which:
-                down_copy(i).start()
+            for item in h_plan[i][low:high]:
+                down_copy(i, *item).start()
 
         @pl.when(~top)
         def _():
-            for i in which:
-                up_copy(i).start()
-
-    def h_wait(*which):
+            for item in h_plan[i][low:high]:
+                up_copy(i, *item).start()
+
+    def h_rows(group):
+        return sum(count * width for _, _, count, width in group)
+
+    def h_wait(i):
         @pl.when(~top)
         def _():
-            for i in which:
-                down_copy(i).wait_recv()
+            rows_wait(hr.at[i, 0], h_rows(h_plan[i]))
 
         @pl.when(~bottom)
         def _():
-            for i in which:
-                up_copy(i).wait_recv()
+            rows_wait(hr.at[i, 1], h_rows(h_plan[i]))
 
     def at(buf, n, r):
         return buf[n, :, pl.ds(r, CHUNK), :]
@@ -415,23 +417,19 @@
         for buf in (sums, e0, e1, e2):
             buf[0, :, pl.ds(TOP, rows), :] = jnp.zeros((blocks, rows, LANES), jnp.float32)
 
-    wait(loads[0])
+    load_wait(0)
     x_send(0)
-    h_send(0)
-    wait(loads[1])
-    wait(loads[2])
+    h_send(0, 0, 1)
+    load_wait(1)
     over_rows(TOP, end, lambda r: put(sums, 1, r, at(src, steps - 1, r) + at(gue, steps - 1, r)))
-    h_send(1, 2)
+    h_send(0, 1)
     x_send(1)
-    wait(loads[3])
-    wait(loads[4])
-    h_send(3, 4)
-    wait(loads[5])
-    wait(loads[6])
-    h_send(5, 6)
-    wait(loads[7])
-    wait(loads[8])
-    h_send(7, 8)
+    load_wait(2)
+    h_send(1)
+    load_wait(3)
+    h_send(2)
+    load_wait(4)
+    h_send(3)
 
     def coefficients(r):
         c = at(coef, COND, r)
@@ -442,125 +440,117 @@
         put(coef, INVK, r, invk)
         put(coef, WK, r, (2.0 * c) * invk)
 
-    h_wait(0, 1, 2)
+    h_wait(0)
     over_rows(*fine_rows, coefficients)
     fine_smooth(gue, u1, steps - 1, steps, fine_rows)
-    h_wait(3, 4)
+    h_wait(1)
     fine_smooth(gue, u1, steps - 3, steps - 1, fine_rows)
+    x_relay(1)
     restrict(half - 1)
     coarse_first(half - 1)
     x_send(2)
     x_edges(0)
     h_send(OLD_GUESS)
-    x_relay(1)
-    h_wait(5, 6)
+    x_relay(0)
+    h_wait(2)
     fine_smooth(gue, u1, steps - 5, steps - 3, fine_rows)
     restrict(half - 2)
     coarse_first(half - 2)
     coarse_sweep(e0, e1, half - 1, 0)
-    x_send(3)
+    x_send_edges(3)
     x_edges(1)
     h_send(OLD_SUM)
-    h_wait(7, 8)
+    h_wait(3)
     fine_smooth(gue, u1, 1, steps - 5, fine_rows)
     restrict(half - 3)
     coarse_first(half - 3)
     coarse_sweep(e0, e1, half - 2, 1)
     coarse_sweep(e1, e2, half - 1, 2)
-    x_send(4)
+    x_send_edges(4)
+    x_send_inner(3, 4)
+    x_edges(2)
+    h_send(OLD_E0)
     h_wait(OLD_GUESS)
-    x_middle(0)
+    x_inner(0)
     fine_smooth(gue, u1, 0, 1, fine_rows)
+    x_relay(2)
 
     h_wait(OLD_SUM)
-    x_middle(1)
+    x_inner(1)
     smooth_before()
     restrict(0)
     coarse_first(0)
-    x_edges(2)
-    h_send(OLD_E0)
+    x_edges(3)
+    h_send(OLD_E1)
     coarse_sweep(e0, e1, 1, 3)
     coarse_sweep(e1, e2, 2, 4)
-    x_relay(2)
+    x_relay(3)
     prolong_odd(half - 1)
     prolong_even(half - 1)
     fine_smooth(u2, u3, steps - 1, steps, late_rows)
     x_send(5)
+    x_edges(4)
+    h_send(OLD_E2)
     prolong_odd(half - 2)
     fine_smooth(u2, u3, steps - 2, steps - 1, late_rows)
     last_residual(steps - 1)
-    x_relay(3)
-    x_edges(3)
-    h_send(OLD_E1)
     h_wait(OLD_E0)
-    x_middle(2)
+    x_inner(2)
     coarse_sweep(e0, e1, 0, 5)
     coarse_sweep(e1, e2, 1, 6)
+    x_relay(4)
     prolong_even(half - 2)
     prolong_odd(half - 3)
     fine_smooth(u2, u3, steps - 4, steps - 2, late_rows)
     h_wait(OLD_E1)
-    x_middle(3)
+    x_inner(3)
     coarse_sweep(e1, e2, 0, 7)
-    x_edges(4)
-    h_send(OLD_E2)
-    x_relay(5)
     over_planes(steps - 3, steps - 1, last_residual)
     prolong_even(1)
     prolong_odd(0)
     fine_smooth(u2, u3, 2, steps - 4, late_rows)
+    x_relay(5)
     over_planes(3, steps - 3, last_residual)
     h_wait(OLD_E2)
-    x_middle(4)
+    x_inner(4)
     over_rows(*late_rows, lambda r: put(u2, 0, r, at(u1, 0, r) + at(e2, 0, r)))
     prolong_even(0)
     fine_smooth(u2, u3, 0, 2, late_rows)
     over_planes(1, 3, last_residual)
     x_edges(5)
-    x_middle(5)
+    x_inner(5)
     last_residual(0)
 
     @pl.when(~last)
     def _():
-        for i in range(len(x_plan)):
-            for piece in direct(i):
-                x_copy(i, piece).wait_send()
-        for i in relayed:
-            to_relay(i, 0, 0).wait_send()
+        rows_wait(xs, rows * len(x_plan))
 
     for device, jobs in relays.items():
 
         @pl.when(tm == device)
         def _():
-            for i in relayed:
-                for slot, final in jobs:
-                    from_relay(i, slot, final).wait_send()
+            for slot, _ in jobs:
+                rows_wait(fs.at[slot], sum(AROUND))
+
+    all_rows = sum(h_rows(group) for group in h_plan)
 
     @pl.when(~bottom)
     def _():
-        for i in range(len(h_plan)):
-            down_copy(i).wait_send()
+        rows_wait(hs.at[0], all_rows)
 
     @pl.when(~top)
     def _():
-        for i in range(len(h_plan)):
-            up_copy(i).wait_send()
+        rows_wait(hs.at[1], all_rows)
 
 
 def store_kernel(steps, rows, blocks, u3, res, field_out, res_out, sem):
-    copies = []
     for k in range(blocks):
         cols = pl.ds(k * LANES, LANES)
-        copies.append(
-            pltpu.make_async_copy(
-                u3.at[pl.ds(1, steps), k, pl.ds(TOP, rows), :], field_out.at[:, :, cols], sem.at[0, k]
-            )
-        )
-        copies.append(pltpu.make_async_copy(res.at[:, k, :, :], res_out.at[:, :, cols], sem.at[1, k]))
-    for c in copies:
-        c.start()
-    for c in copies:
-        c.wait()
+        own = u3.at[pl.ds(1, steps), k, pl.ds(TOP, rows), :]
+        pltpu.make_async_copy(own, field_out.at[:, :, cols], sem.at[0]).start()
+        pltpu.make_async_copy(res.at[:, k, :, :], res_out.at[:, :, cols], sem.at[1]).start()
+    pltpu.make_async_copy(field_out, field_out, sem.at[0]).wait()
+    pltpu.make_async_copy(res_out, res_out, sem.at[1]).wait()
 
 
 def shards(source, guess, start_state, conduct):
@@ -595,15 +585,14 @@
             planes(steps),
             planes(5),
             planes(2),
-            pltpu.VMEM((2, 4, blocks, rows - 2 * EDGE, LANES), f32),
-            pltpu.SemaphoreType.DMA((11, blocks)),
-            pltpu.SemaphoreType.DMA((6, 3)),
-            pltpu.SemaphoreType.DMA((6, 3)),
-            pltpu.SemaphoreType.DMA((4,)),
-            pltpu.SemaphoreType.DMA((2, 4)),
-            pltpu.SemaphoreType.DMA((2, 4)),
-            pltpu.SemaphoreType.DMA((14, 2)),
-            pltpu.SemaphoreType.DMA((14, 2)),
+            pltpu.VMEM((2, 6, blocks, max(AROUND), LANES), f32),
+            pltpu.SemaphoreType.DMA((7,)),
+            pltpu.SemaphoreType.DMA,
+            pltpu.SemaphoreType.DMA((6, 2)),
+            pltpu.SemaphoreType.DMA((2, 6)),
+            pltpu.SemaphoreType.DMA((2,)),
+            pltpu.SemaphoreType.DMA((2,)),
+            pltpu.SemaphoreType.DMA((9, 2)),
         ],
         compiler_params=pltpu.CompilerParams(
             collective_id=0, has_side_effects=True, vmem_limit_bytes=44 * 1024 * 1024
@@ -615,7 +604,7 @@
         out_shape=(jax.ShapeDtypeStruct(source.shape, f32), jax.ShapeDtypeStruct(source.shape, f32)),
         in_specs=[vmem, vmem],
         out_specs=(hbm, hbm),
-        scratch_shapes=[pltpu.SemaphoreType.DMA((2, blocks))],
+        scratch_shapes=[pltpu.SemaphoreType.DMA((2,))],
         compiler_params=pltpu.CompilerParams(vmem_limit_bytes=16 * 1024 * 1024),
         name="store",
     )(u3, res)

time: 38.3 us -> 35.4 us (0.924); the launches traced: 38.2 us -> 34.8 us
  Pallas kernels: 37.4 us -> 34 us
    pallas_call x1, Pallas kernels: 35.3 us -> 32 us  [shards(): pl.pallas_call(functools.partial(cycle_kernel, steps, rows, blocks), out_...]
where the time goes in v4:
time: 35.4 us; the launch traced here: 34.8 us
  Pallas kernels  34 us (96%)
  between operations  0.8 us (2%)
    pallas_call x1, Pallas kernels, shards(): pl.pallas_call(functools.partial(cycle_kernel, steps, rows, blocks), out_...  32 us
    pallas_call x1, Pallas kernels, shards(): pl.pallas_call(functools.partial(store_kernel, steps, rows, blocks), out_...  2.01 us

profile of v4, /device:TPU:100, one launch (start us, length us, event | category | flops | bytes accessed | tf_op | source)
XLA Modules:
  0.0 34.8 jit_solution(6062232071916072295)
XLA Ops:
  0.6 32.0 %cycle.1 = (f32[9,8,96,128]{3,2,1,0:T(8,128)S(1)}, f32[8,8,64,128]{3,2,1,0:T(8,128)S(1)}) custom-call(f32[8,64,1024]{2,1,0:T(8,128)} %source_hbm.1, f32[8,64,1024]{2,1,0:T(8,128)} %guess_hbm.1, f32[64,1024]{1,0:T(8,128)} %start_hbm.1, f32[64,1024]{1,0:T(8,128)} %cond_hbm.1), custom_call_target="tpu_custom_call" | custom-call | tf_op jit(solution)/shard_map/cycle/pallas_call | solution.py:568
  32.6 2.0 %store.1 = (f32[8,64,1024]{2,1,0:T(8,128)}, f32[8,64,1024]{2,1,0:T(8,128)}) custom-call(f32[9,8,96,128]{3,2,1,0:T(8,128)S(1)} %get-tuple-element.4.u3, f32[8,8,64,128]{3,2,1,0:T(8,128)S(1)} %get-tuple-element.5.res), custom_call_target="tpu_custom_call" | custom-call | tf_op jit(solution)/shard_map/store/pallas_call | solution.py:602

commit v5 on v4

--- a/solution.py
+++ b/solution.py
@@ -14,7 +14,7 @@
 TOP = 16
 CHUNK = 8
 EDGE = (12, 12, 8, 8, 8, 8)
-AROUND = (8, 16, 8, 12, 12, 16)
+AROUND = (8, 16, 8, 12, 16, 16)
 
 
 def cycle_kernel(
@@ -44,6 +44,7 @@
     xr,
     lr,
     fs,
+    meet,
     hs,
     hr,
 ):
@@ -54,6 +55,18 @@
     first, last = tm == 0, tm == n_tm - 1
     top, bottom = sp == 0, sp == n_sp - 1
     COND, INV, W, INVK, WK = range(5)
+
+    barrier = pltpu.get_barrier_semaphore()
+
+    def greet(cond, axis, index):
+        @pl.when(cond)
+        def _():
+            pl.semaphore_signal(barrier, inc=1, device_id={axis: index}, device_id_type=MESH)
+
+    greet(~first, "tm", tm - 1)
+    greet(~last, "tm", tm + 1)
+    greet(~top, "space", sp - 1)
+    greet(~bottom, "space", sp + 1)
 
     def rows_wait(sem, count):
         planes = next(n for n in range(1, count + 1) if count % n == 0 and count // n <= end)
@@ -98,21 +111,10 @@
             for c in load(5 + i, start_hbm, None, buf, 0, 1):
                 c.start()
 
-    barrier = pltpu.get_barrier_semaphore()
-
-    def greet(cond, axis, index):
-        @pl.when(cond)
-        def _():
-            pl.semaphore_signal(barrier, inc=1, device_id={axis: index}, device_id_type=MESH)
-
-    for other in range(n_tm):
-        greet((tm != other) & (tm + other != 2), "tm", other)
-    greet(~top, "space", sp - 1)
-    greet(~bottom, "space", sp + 1)
     one = jnp.int32(1)
     zero = jnp.int32(0)
-    peers = jnp.where((tm == 1) | (tm == 3), one * 3, one * 2)
-    pl.semaphore_wait(barrier, peers + jnp.where(top, zero, one) + jnp.where(bottom, zero, one))
+    peers = [jnp.where(edge, zero, one) for edge in (first, last, top, bottom)]
+    pl.semaphore_wait(barrier, peers[0] + peers[1] + peers[2] + peers[3])
 
     x_plan = [(gue, steps), (sums, 1), (e0, half), (e1, half), (e2, half), (u3, steps)]
     ways = {0: (3, 0), 1: (3, 1), 2: (1, 0)}
@@ -163,6 +165,7 @@
             x_copy(i, FIRST_ROWS).start()
             x_copy(i, LAST_ROWS).start()
 
+    def x_send_around(i):
         for sender, way in ways.items():
 
             @pl.when(tm == sender)
@@ -175,8 +178,19 @@
             for i in which:
                 x_copy(i, INNER).start()
 
+    def x_tell(device):
+        @pl.when(tm == device)
+        def _():
+            pl.semaphore_signal(meet, inc=1, device_id={"tm": device - 1}, device_id_type=MESH)
+
+    def x_hear(device):
+        @pl.when(tm == device)
+        def _():
+            pl.semaphore_wait(meet, 1)
+
     def x_send(i):
         x_send_edges(i)
+        x_send_around(i)
         x_send_inner(i)
 
     def x_relay(i):
@@ -386,7 +400,7 @@
     def last_residual(n):
         def chunk(r):
             v, s = with_sum(u3, n + 1, r)
-            rest = at(src, n, r) + (at(u3, n, r) - v)
+            rest = at(src, n, r) - v if isinstance(n, int) and n == 0 else at(src, n, r) + (at(u3, n, r) - v)
             res[n, :, pl.ds(r - TOP, CHUNK), :] = rest - at(coef, COND, r) * (4.0 * v - s)
 
         over_rows(TOP, end, chunk)
@@ -417,19 +431,27 @@
         for buf in (sums, e0, e1, e2):
             buf[0, :, pl.ds(TOP, rows), :] = jnp.zeros((blocks, rows, LANES), jnp.float32)
 
+    x_tell(2)
     load_wait(0)
-    x_send(0)
+    x_send_edges(0)
+    x_send_inner(0)
     h_send(0, 0, 1)
     load_wait(1)
     over_rows(TOP, end, lambda r: put(sums, 1, r, at(src, steps - 1, r) + at(gue, steps - 1, r)))
     h_send(0, 1)
-    x_send(1)
+    x_send_edges(1)
+    x_send_inner(1)
+    x_hear(1)
+    x_tell(1)
     load_wait(2)
     h_send(1)
     load_wait(3)
     h_send(2)
     load_wait(4)
     h_send(3)
+    x_hear(0)
+    x_send_around(1)
+    x_send_around(0)
 
     def coefficients(r):
         c = at(coef, COND, r)
@@ -458,6 +480,7 @@
     coarse_first(half - 2)
     coarse_sweep(e0, e1, half - 1, 0)
     x_send_edges(3)
+    x_send_around(3)
     x_edges(1)
     h_send(OLD_SUM)
     h_wait(3)
@@ -467,6 +490,7 @@
     coarse_sweep(e0, e1, half - 2, 1)
     coarse_sweep(e1, e2, half - 1, 2)
     x_send_edges(4)
+    x_send_around(4)
     x_send_inner(3, 4)
     x_edges(2)
     h_send(OLD_E0)
@@ -482,9 +506,9 @@
     coarse_first(0)
     x_edges(3)
     h_send(OLD_E1)
+    x_relay(3)
     coarse_sweep(e0, e1, 1, 3)
     coarse_sweep(e1, e2, 2, 4)
-    x_relay(3)
     prolong_odd(half - 1)
     prolong_even(half - 1)
     fine_smooth(u2, u3, steps - 1, steps, late_rows)
@@ -506,10 +530,10 @@
     x_inner(3)
     coarse_sweep(e1, e2, 0, 7)
     over_planes(steps - 3, steps - 1, last_residual)
+    x_relay(5)
     prolong_even(1)
     prolong_odd(0)
     fine_smooth(u2, u3, 2, steps - 4, late_rows)
-    x_relay(5)
     over_planes(3, steps - 3, last_residual)
     h_wait(OLD_E2)
     x_inner(4)
@@ -517,9 +541,15 @@
     prolong_even(0)
     fine_smooth(u2, u3, 0, 2, late_rows)
     over_planes(1, 3, last_residual)
+    last_residual(0)
     x_edges(5)
     x_inner(5)
-    last_residual(0)
+
+    def add_before(r):
+        part = pl.ds(r - TOP, CHUNK)
+        res[0, :, part, :] = res[0, :, part, :] + at(u3, 0, r)
+
+    over_rows(TOP, end, add_before)
 
     @pl.when(~last)
     def _():
@@ -591,6 +621,7 @@
             pltpu.SemaphoreType.DMA((6, 2)),
             pltpu.SemaphoreType.DMA((2, 6)),
             pltpu.SemaphoreType.DMA((2,)),
+            pltpu.SemaphoreType.REGULAR,
             pltpu.SemaphoreType.DMA((2,)),
             pltpu.SemaphoreType.DMA((9, 2)),
         ],

time: 35.4 us -> 34.6 us (0.977)
  Pallas kernels: 34 us -> 33.5 us
    pallas_call x1, Pallas kernels: 32 us -> 31.5 us  [shards(): pl.pallas_call(functools.partial(cycle_kernel, steps, rows, blocks), out_...]
where the time goes in v5:
time: 34.6 us; the launch traced here: 34.3 us
  Pallas kernels  33.5 us (97%)
  between operations  0.8 us (2%)
    pallas_call x1, Pallas kernels, shards(): pl.pallas_call(functools.partial(cycle_kernel, steps, rows, blocks), out_...  31.5 us
    pallas_call x1, Pallas kernels, shards(): pl.pallas_call(functools.partial(store_kernel, steps, rows, blocks), out_...  2.01 us

profile of v5, /device:TPU:100, one launch (start us, length us, event | category | flops | bytes accessed | tf_op | source)
XLA Modules:
  0.0 34.3 jit_solution(6103037322510125327)
XLA Ops:
  0.6 31.5 %cycle.1 = (f32[9,8,96,128]{3,2,1,0:T(8,128)S(1)}, f32[8,8,64,128]{3,2,1,0:T(8,128)S(1)}) custom-call(f32[8,64,1024]{2,1,0:T(8,128)} %source_hbm.1, f32[8,64,1024]{2,1,0:T(8,128)} %guess_hbm.1, f32[64,1024]{1,0:T(8,128)} %start_hbm.1, f32[64,1024]{1,0:T(8,128)} %cond_hbm.1), custom_call_target="tpu_custom_call" | custom-call | tf_op jit(solution)/shard_map/cycle/pallas_call | solution.py:598
  32.1 2.0 %store.1 = (f32[8,64,1024]{2,1,0:T(8,128)}, f32[8,64,1024]{2,1,0:T(8,128)}) custom-call(f32[9,8,96,128]{3,2,1,0:T(8,128)S(1)} %get-tuple-element.4.u3, f32[8,8,64,128]{3,2,1,0:T(8,128)S(1)} %get-tuple-element.5.res), custom_call_target="tpu_custom_call" | custom-call | tf_op jit(solution)/shard_map/store/pallas_call | solution.py:633

commit v6 on v5

--- a/solution.py
+++ b/solution.py
@@ -14,7 +14,7 @@
 TOP = 16
 CHUNK = 8
 EDGE = (12, 12, 8, 8, 8, 8)
-AROUND = (8, 16, 8, 12, 16, 16)
+AROUND = (8, 16, 8, 12, 16, 12)
 
 
 def cycle_kernel(
@@ -235,8 +235,8 @@
         return pltpu.make_async_remote_copy(
             src_ref=buf.at[pl.ds(plane, count), :, pl.ds(end - width, width), :],
             dst_ref=buf.at[pl.ds(plane, count), :, pl.ds(TOP - width, width), :],
-            send_sem=hs.at[0],
-            recv_sem=hr.at[i, 0],
+            send_sem=hs,
+            recv_sem=hr.at[i],
             device_id={"space": sp + 1},
             device_id_type=MESH,
         )
@@ -245,8 +245,8 @@
         return pltpu.make_async_remote_copy(
             src_ref=buf.at[pl.ds(plane, count), :, pl.ds(TOP, width), :],
             dst_ref=buf.at[pl.ds(plane, count), :, pl.ds(end, width), :],
-            send_sem=hs.at[1],
-            recv_sem=hr.at[i, 1],
+            send_sem=hs,
+            recv_sem=hr.at[i],
             device_id={"space": sp - 1},
             device_id_type=MESH,
         )
@@ -265,14 +265,17 @@
     def h_rows(group):
         return sum(count * width for _, _, count, width in group)
 
+    def h_count(sem, count):
+        @pl.when(top | bottom)
+        def _():
+            rows_wait(sem, count)
+
+        @pl.when(~top & ~bottom)
+        def _():
+            rows_wait(sem, 2 * count)
+
     def h_wait(i):
-        @pl.when(~top)
-        def _():
-            rows_wait(hr.at[i, 0], h_rows(h_plan[i]))
-
-        @pl.when(~bottom)
-        def _():
-            rows_wait(hr.at[i, 1], h_rows(h_plan[i]))
+        h_count(hr.at[i], h_rows(h_plan[i]))
 
     def at(buf, n, r):
         return buf[n, :, pl.ds(r, CHUNK), :]
@@ -430,6 +433,14 @@
     def _():
         for buf in (sums, e0, e1, e2):
             buf[0, :, pl.ds(TOP, rows), :] = jnp.zeros((blocks, rows, LANES), jnp.float32)
+
+    odd = lax.rem(sp, 2) == 1
+
+    def x_send_inner_if(turn, *which):
+        @pl.when(turn & ~last)
+        def _():
+            for i in which:
+                x_copy(i, INNER).start()
 
     x_tell(2)
     load_wait(0)
@@ -491,7 +502,7 @@
     coarse_sweep(e1, e2, half - 1, 2)
     x_send_edges(4)
     x_send_around(4)
-    x_send_inner(3, 4)
+    x_send_inner_if(~odd, 3, 4)
     x_edges(2)
     h_send(OLD_E0)
     h_wait(OLD_GUESS)
@@ -504,6 +515,7 @@
     smooth_before()
     restrict(0)
     coarse_first(0)
+    x_send_inner_if(odd, 3, 4)
     x_edges(3)
     h_send(OLD_E1)
     x_relay(3)
@@ -562,23 +574,18 @@
             for slot, _ in jobs:
                 rows_wait(fs.at[slot], sum(AROUND))
 
-    all_rows = sum(h_rows(group) for group in h_plan)
-
-    @pl.when(~bottom)
-    def _():
-        rows_wait(hs.at[0], all_rows)
-
-    @pl.when(~top)
-    def _():
-        rows_wait(hs.at[1], all_rows)
+    h_count(hs, sum(h_rows(group) for group in h_plan))
 
 
 def store_kernel(steps, rows, blocks, u3, res, field_out, res_out, sem):
-    for k in range(blocks):
-        cols = pl.ds(k * LANES, LANES)
-        own = u3.at[pl.ds(1, steps), k, pl.ds(TOP, rows), :]
-        pltpu.make_async_copy(own, field_out.at[:, :, cols], sem.at[0]).start()
-        pltpu.make_async_copy(res.at[:, k, :, :], res_out.at[:, :, cols], sem.at[1]).start()
+    some = steps // 4
+    for low in range(0, steps, some):
+        for k in range(blocks):
+            cols = pl.ds(k * LANES, LANES)
+            own = u3.at[pl.ds(1 + low, some), k, pl.ds(TOP, rows), :]
+            out = res.at[pl.ds(low, some), k, :, :]
+            pltpu.make_async_copy(own, field_out.at[pl.ds(low, some), :, cols], sem.at[0]).start()
+            pltpu.make_async_copy(out, res_out.at[pl.ds(low, some), :, cols], sem.at[1]).start()
     pltpu.make_async_copy(field_out, field_out, sem.at[0]).wait()
     pltpu.make_async_copy(res_out, res_out, sem.at[1]).wait()
 
@@ -622,8 +629,8 @@
             pltpu.SemaphoreType.DMA((2, 6)),
             pltpu.SemaphoreType.DMA((2,)),
             pltpu.SemaphoreType.REGULAR,
-            pltpu.SemaphoreType.DMA((2,)),
-            pltpu.SemaphoreType.DMA((9, 2)),
+            pltpu.SemaphoreType.DMA,
+            pltpu.SemaphoreType.DMA((9,)),
         ],
         compiler_params=pltpu.CompilerParams(
             collective_id=0, has_side_effects=True, vmem_limit_bytes=44 * 1024 * 1024

time: 34.6 us -> 34.3 us (level)
  Pallas kernels: 33.5 us -> 33 us
    pallas_call x1, Pallas kernels: 31.5 us -> 31 us  [shards(): pl.pallas_call(functools.partial(cycle_kernel, steps, rows, blocks), out_...]
where the time goes in v6:
time: 34.3 us; the launch traced here: 33.8 us
  Pallas kernels  33 us (96%)
  between operations  0.8 us (2%)
    pallas_call x1, Pallas kernels, shards(): pl.pallas_call(functools.partial(cycle_kernel, steps, rows, blocks), out_...  31 us
    pallas_call x1, Pallas kernels, shards(): pl.pallas_call(functools.partial(store_kernel, steps, rows, blocks), out_...  1.98 us

profile of v6, /device:TPU:100, one launch (start us, length us, event | category | flops | bytes accessed | tf_op | source)
XLA Modules:
  0.0 33.8 jit_solution(2656423817137057792)
XLA Ops:
  0.6 31.0 %cycle.1 = (f32[9,8,96,128]{3,2,1,0:T(8,128)S(1)}, f32[8,8,64,128]{3,2,1,0:T(8,128)S(1)}) custom-call(f32[8,64,1024]{2,1,0:T(8,128)} %source_hbm.1, f32[8,64,1024]{2,1,0:T(8,128)} %guess_hbm.1, f32[64,1024]{1,0:T(8,128)} %start_hbm.1, f32[64,1024]{1,0:T(8,128)} %cond_hbm.1), custom_call_target="tpu_custom_call" | custom-call | tf_op jit(solution)/shard_map/cycle/pallas_call | solution.py:605
  31.6 2.0 %store.1 = (f32[8,64,1024]{2,1,0:T(8,128)}, f32[8,64,1024]{2,1,0:T(8,128)}) custom-call(f32[9,8,96,128]{3,2,1,0:T(8,128)S(1)} %get-tuple-element.4.u3, f32[8,8,64,128]{3,2,1,0:T(8,128)S(1)} %get-tuple-element.5.res), custom_call_target="tpu_custom_call" | custom-call | tf_op jit(solution)/shard_map/store/pallas_call | solution.py:640

commit v7 on v6

--- a/solution.py
+++ b/solution.py
@@ -14,7 +14,7 @@
 TOP = 16
 CHUNK = 8
 EDGE = (12, 12, 8, 8, 8, 8)
-AROUND = (8, 16, 8, 12, 16, 12)
+AROUND = (8, 20, 8, 12, 16, 12)
 
 
 def cycle_kernel(
@@ -516,11 +516,11 @@
     restrict(0)
     coarse_first(0)
     x_send_inner_if(odd, 3, 4)
+    coarse_sweep(e0, e1, 1, 3)
+    coarse_sweep(e1, e2, 2, 4)
     x_edges(3)
     h_send(OLD_E1)
     x_relay(3)
-    coarse_sweep(e0, e1, 1, 3)
-    coarse_sweep(e1, e2, 2, 4)
     prolong_odd(half - 1)
     prolong_even(half - 1)
     fine_smooth(u2, u3, steps - 1, steps, late_rows)

time: 34.3 us -> 34.4 us (level); the launches traced: 33.8 us -> 34.3 us
  Pallas kernels: 33 us -> 33.5 us
    pallas_call x1, Pallas kernels: 31 us -> 31.5 us  [shards(): pl.pallas_call(functools.partial(cycle_kernel, steps, rows, blocks), out_...]
where the time goes in v7:
time: 34.4 us; the launch traced here: 34.3 us
  Pallas kernels  33.5 us (97%)
  between operations  0.8 us (2%)
    pallas_call x1, Pallas kernels, shards(): pl.pallas_call(functools.partial(cycle_kernel, steps, rows, blocks), out_...  31.5 us
    pallas_call x1, Pallas kernels, shards(): pl.pallas_call(functools.partial(store_kernel, steps, rows, blocks), out_...  1.98 us

profile of v7, /device:TPU:100, one launch (start us, length us, event | category | flops | bytes accessed | tf_op | source)
XLA Modules:
  0.0 34.3 jit_solution(15474843137060434641)
XLA Ops:
  0.6 31.5 %cycle.1 = (f32[9,8,96,128]{3,2,1,0:T(8,128)S(1)}, f32[8,8,64,128]{3,2,1,0:T(8,128)S(1)}) custom-call(f32[8,64,1024]{2,1,0:T(8,128)} %source_hbm.1, f32[8,64,1024]{2,1,0:T(8,128)} %guess_hbm.1, f32[64,1024]{1,0:T(8,128)} %start_hbm.1, f32[64,1024]{1,0:T(8,128)} %cond_hbm.1), custom_call_target="tpu_custom_call" | custom-call | tf_op jit(solution)/shard_map/cycle/pallas_call | solution.py:605
  32.2 2.0 %store.1 = (f32[8,64,1024]{2,1,0:T(8,128)}, f32[8,64,1024]{2,1,0:T(8,128)}) custom-call(f32[9,8,96,128]{3,2,1,0:T(8,128)S(1)} %get-tuple-element.4.u3, f32[8,8,64,128]{3,2,1,0:T(8,128)S(1)} %get-tuple-element.5.res), custom_call_target="tpu_custom_call" | custom-call | tf_op jit(solution)/shard_map/store/pallas_call | solution.py:640

commit v8 on v7

--- a/solution.py
+++ b/solution.py
@@ -541,8 +541,8 @@
     h_wait(OLD_E1)
     x_inner(3)
     coarse_sweep(e1, e2, 0, 7)
+    x_relay(5)
     over_planes(steps - 3, steps - 1, last_residual)
-    x_relay(5)
     prolong_even(1)
     prolong_odd(0)
     fine_smooth(u2, u3, 2, steps - 4, late_rows)

time: 34.4 us -> 34.4 us (level)
  no operation moved by 1% of the time
where the time goes in v8:
time: 34.4 us; the launch traced here: 34.3 us
  Pallas kernels  33.5 us (97%)
  between operations  0.8 us (2%)
    pallas_call x1, Pallas kernels, shards(): pl.pallas_call(functools.partial(cycle_kernel, steps, rows, blocks), out_...  31.5 us
    pallas_call x1, Pallas kernels, shards(): pl.pallas_call(functools.partial(store_kernel, steps, rows, blocks), out_...  1.98 us

profile of v8, /device:TPU:100, one launch (start us, length us, event | category | flops | bytes accessed | tf_op | source)
XLA Modules:
  0.0 34.3 jit_solution(12004519448381353489)
XLA Ops:
  0.6 31.5 %cycle.1 = (f32[9,8,96,128]{3,2,1,0:T(8,128)S(1)}, f32[8,8,64,128]{3,2,1,0:T(8,128)S(1)}) custom-call(f32[8,64,1024]{2,1,0:T(8,128)} %source_hbm.1, f32[8,64,1024]{2,1,0:T(8,128)} %guess_hbm.1, f32[64,1024]{1,0:T(8,128)} %start_hbm.1, f32[64,1024]{1,0:T(8,128)} %cond_hbm.1), custom_call_target="tpu_custom_call" | custom-call | tf_op jit(solution)/shard_map/cycle/pallas_call | solution.py:605
  32.2 2.0 %store.1 = (f32[8,64,1024]{2,1,0:T(8,128)}, f32[8,64,1024]{2,1,0:T(8,128)}) custom-call(f32[9,8,96,128]{3,2,1,0:T(8,128)S(1)} %get-tuple-element.4.u3, f32[8,8,64,128]{3,2,1,0:T(8,128)S(1)} %get-tuple-element.5.res), custom_call_target="tpu_custom_call" | custom-call | tf_op jit(solution)/shard_map/store/pallas_call | solution.py:640
